TPU v7x, 768 devices: a whole 4x8x12 slice. The times are simulated.
768 devices in a mesh: gx: 8 (over y), gy: 8 (over z_lo, core), gz: 12 (over z_hi, x).
Axes of the slice: x: 4, y: 8, z: 12 (z_hi: 3, z_lo: 4; z = z_hi * 4 + z_lo), core: 2. Of those that a mesh axis runs over, the one named last changes fastest.
Arguments:
- positions: float32 [3, 16, 32, 24, 128], P(None, 'gx', 'gy', 'gz'), may hold values from 0 to 1
- type_ids: int32 [16, 32, 24, 128], P('gx', 'gy', 'gz'), may hold values from 0 to 1
- counts: int32 [16, 32, 24], P('gx', 'gy', 'gz'), may hold values from 64 to 128
- type_charge: float32 [2], replicated, may hold values from -1 to 1
- type_sigma: float32 [2], replicated, may hold values from 0.2 to 0.35
- type_epsilon: float32 [2], replicated, may hold values from 0.05 to 0.5
Outputs:
- forces: float32 [3, 16, 32, 24, 128], P(None, 'gx', 'gy', 'gz')
- totals: float32 [2], replicated
All inputs are finite; a program needn't handle non-finite values.
Results may differ from a plain program's by a relative error of at most 0.0003.
Values sent between devices are 32-bit elements; how exact they have to be, the bound alone decides.
No kernel may reach another device: no remote copies, remote signals or barrier semaphores. Data moves between devices by JAX's collectives and lax.ppermute only.
A program may use at most 64 MiB of HBM per device.

v0:
```python
import functools

import jax
import jax.numpy as jnp
from jax import lax
from jax.sharding import Mesh
from jax.sharding import PartitionSpec as P

GY = ("gy_0", "gy_1")
GZ = ("gz_0", "gz_1")
GX_GY_GZ = ("gx", "gy_0", "gy_1", "gz_0", "gz_1")


soft_core = 0.09
corner_pairs = [
    (first_corner, second_corner)
    for first_corner in range(8)
    for second_corner in range(8)
    if first_corner & second_corner == 0 and first_corner <= second_corner
]


def passed_along(value, axis, steps):
    count = lax.axis_size(axis)
    pairs = [(source, (source + steps) % count) for source in range(count)]
    return lax.ppermute(value, axis, pairs)


def one_axis_at_a_time(value, axes):
    return functools.reduce(lax.psum, axes, value)


def corner_of(which):
    return (which & 1, which >> 1 & 1, which >> 2 & 1)


def atom_table(positions, type_ids, counts, type_charge, type_sigma, type_epsilon):
    type_count = type_charge.shape[0]
    kinds_shape = (type_count, 1, 1, 1, 1)
    onehot = (
        type_ids[None] == jnp.arange(type_count, dtype=jnp.int32).reshape(kinds_shape)
    ).astype(jnp.float32)
    charge = jnp.sum(onehot * type_charge.reshape(kinds_shape), 0)
    sigma_atom = jnp.sum(onehot * type_sigma.reshape(kinds_shape), 0)
    depth_atom = jnp.sum(onehot * jnp.sqrt(type_epsilon).reshape(kinds_shape), 0)
    slots = lax.broadcasted_iota(jnp.int32, type_ids.shape, 3)
    occupied = (slots < counts[..., None]).astype(jnp.float32)
    return jnp.stack(
        [positions[0], positions[1], positions[2], charge, sigma_atom, depth_atom, occupied]
    )


def pair_terms(first, second, offset, selfpair):
    displace = second[:3, :, None, :] - first[:3, :, :, None] + offset[:, None, None, None]
    dist_sq = jnp.sum(displace * displace, 0)
    width_atoms = first.shape[-1]
    live_mask = first[6][:, :, None] * second[6][:, None, :] * (dist_sq < 1.0).astype(jnp.float32)
    if selfpair:
        ordered = (
            lax.broadcasted_iota(jnp.int32, (width_atoms, width_atoms), 0)
            < lax.broadcasted_iota(jnp.int32, (width_atoms, width_atoms), 1)
        ).astype(jnp.float32)
        live_mask = live_mask * ordered[None]
    sigma_pair = 0.5 * (first[4][:, :, None] + second[4][:, None, :])
    depth_pair = first[5][:, :, None] * second[5][:, None, :]
    coulomb = first[3][:, :, None] * second[3][:, None, :]
    soft_sq = dist_sq + soft_core
    inverse = lax.rsqrt(soft_sq)
    ratio_six = (sigma_pair * sigma_pair / soft_sq) ** 3
    ratio_twelve = ratio_six * ratio_six
    value_here = 4.0 * depth_pair * (ratio_twelve - ratio_six) + coulomb * inverse
    slope_here = (
        4.0 * depth_pair * (6.0 * ratio_six - 12.0 * ratio_twelve) - coulomb * inverse
    ) * inverse
    cut_sq = 1.0 + soft_core
    cut_len = cut_sq**0.5
    cut_six = (sigma_pair * sigma_pair / cut_sq) ** 3
    cut_twelve = cut_six * cut_six
    value_cut = 4.0 * depth_pair * (cut_twelve - cut_six) + coulomb / cut_len
    slope_cut = (
        4.0 * depth_pair * (6.0 * cut_six - 12.0 * cut_twelve) - coulomb / cut_len
    ) / cut_len
    energy = live_mask * (value_here - value_cut - (soft_sq * inverse - cut_len) * slope_cut)
    slope = live_mask * (slope_here - slope_cut) * inverse
    weighted = slope[None] * displace
    return (jnp.sum(weighted, 3), -jnp.sum(weighted, 2), jnp.sum(energy), jnp.sum(slope * dist_sq))


def per_device(positions, type_ids, counts, type_charge, type_sigma, type_epsilon):
    features = atom_table(positions, type_ids, counts, type_charge, type_sigma, type_epsilon)
    size_x, size_y, size_z, width_atoms = features.shape[1:]
    extended = jnp.concatenate([features, passed_along(features[:, :1], "gx", -1)], 1)
    extended = jnp.concatenate([extended, passed_along(extended[:, :, :1], GY, -1)], 2)
    extended = jnp.concatenate([extended, passed_along(extended[:, :, :, :1], GZ, -1)], 3)
    cell_rows = size_x * size_y * size_z

    def slabs_of(which):
        shift_x, shift_y, shift_z = corner_of(which)
        view = extended[
            :, shift_x : shift_x + size_x, shift_y : shift_y + size_y, shift_z : shift_z + size_z
        ]
        return view.reshape((7, cell_rows, width_atoms))

    reaction = jnp.zeros((3, size_x + 1, size_y + 1, size_z + 1, width_atoms), jnp.float32)

    def deposit(reaction, force_rows, which):
        shift_x, shift_y, shift_z = corner_of(which)
        grid = force_rows.reshape((3, size_x, size_y, size_z, width_atoms))
        return reaction.at[
            :, shift_x : shift_x + size_x, shift_y : shift_y + size_y, shift_z : shift_z + size_z
        ].add(grid)

    energy = jnp.float32(0.0)
    virial = jnp.float32(0.0)
    for first_corner, second_corner in corner_pairs:
        offset = jnp.array(
            [float(a - b) for a, b in zip(corner_of(second_corner), corner_of(first_corner))],
            jnp.float32,
        )
        selfpair = first_corner == second_corner
        force_first, force_second, energies, virials = pair_terms(
            slabs_of(first_corner), slabs_of(second_corner), offset, selfpair
        )
        reaction = deposit(reaction, force_first, first_corner)
        reaction = deposit(reaction, force_second, second_corner)
        energy = energy + energies
        virial = virial + virials
    returned = passed_along(reaction[:, :, :, size_z:], GZ, 1)
    reaction = reaction[:, :, :, :size_z].at[:, :, :, :1].add(returned)
    returned = passed_along(reaction[:, :, size_y:], GY, 1)
    reaction = reaction[:, :, :size_y].at[:, :, :1].add(returned)
    returned = passed_along(reaction[:, size_x:], "gx", 1)
    forces = reaction[:, :size_x].at[:, :1].add(returned)
    summed = (one_axis_at_a_time(energy, GX_GY_GZ), one_axis_at_a_time(virial, GX_GY_GZ))
    normaliser = 1.0 / (
        size_x
        * lax.axis_size("gx")
        * size_y
        * lax.axis_size(GY)
        * size_z
        * lax.axis_size(GZ)
        * width_atoms
    )
    totals = jnp.stack([summed[0], summed[1]]) * normaliser
    return (forces, totals)


def solution(mesh):
    split = Mesh(
        mesh.devices.reshape(mesh.shape["gx"], 4, 2, 3, 4), ("gx", "gy_0", "gy_1", "gz_0", "gz_1")
    )
    placed = (P(None, "gx", GY, GZ, None), P("gx", GY, GZ, None), P("gx", GY, GZ), P(), P(), P())
    return jax.shard_map(
        per_device,
        mesh=split,
        in_specs=placed,
        out_specs=(P(None, "gx", GY, GZ, None), P()),
        check_vma=False,
    )
```

profile of v0, /device:TPU:66, one launch (start us, length us, event | category | flops | bytes accessed | tf_op | source)
XLA Modules:
  0.0 200.6 jit_solution(13585261196587144933)
XLA Ops:
  0.7 0.7 copy.33
  1.4 0.7 sqrt.3
  2.1 0.7 constant_dynamic-update-slice_fusion.4
  2.8 0.8 copy.32
  3.6 0.8 select_reduce_fusion.2
  4.5 5.4 %collective-permute-start = (f32[7,1,4,2,128]{4,3,2,1,0:T(2,128)S(1)}, f32[7,1,4,2,128]{4,3,2,1,0:T(2,128)S(1)}, u32[]{:S(2)}, u32[]{:S(2)}) collective-permute-start(f32[7,1,4,2,128]{4,3,2,1,0:T(2,128)S(1)} %slice.1661), channel_id=1, source_target_pairs={{0,672},{96,0},{192,96},{288,192},{384,288},{480,384},{576,480},{6... | collective-permute-start | bytes 86024 | tf_op jit(solution)/shard_map/ppermute | solution.py:26
  10.1 1.3 collective-permute-done
  11.4 1.9 collective-permute-start.1
  13.4 1.5 collective-permute-done.1
  15.0 2.4 %collective-permute-start.2 = (f32[7,3,5,1,128]{4,3,2,1,0:T(1,128)S(1)}, f32[7,3,5,1,128]{4,3,2,1,0:T(1,128)S(1)}, u32[]{:S(2)}, u32[]{:S(2)}) collective-permute-start(f32[7,3,5,1,128]{4,3,2,1,0:T(1,128)S(1)} %slice.1680), channel_id=1, source_target_pairs={{0,11},{1,0},{2,1},{3,2},{4,3},{5,4},{6,5},{7,6},{8,7},{9,8},{10,9... | collective-permute-start | bytes 161288 | tf_op jit(solution)/shard_map/ppermute | solution.py:26
  17.4 3.5 %collective-permute-done.2 = f32[7,3,5,1,128]{4,3,2,1,0:T(1,128)S(1)} collective-permute-done((f32[7,3,5,1,128]{4,3,2,1,0:T(1,128)S(1)}, f32[7,3,5,1,128]{4,3,2,1,0:T(1,128)S(1)}, u32[]{:S(2)}, u32[]{:S(2)}) %collective-permute-start.2) | collective-permute-done | bytes 53792 | tf_op jit(solution)/shard_map/ppermute | solution.py:26
  21.2 3.5 %multiply_reduce_fusion.1 = (f32[16,128,128]{2,1,0:T(8,128)S(1)}, f32[16,128,128]{2,1,0:T(8,128)S(1)}, f32[16,128,128]{2,1,0:T(8,128)S(1)}, f32[16,128,128]{2,1,0:T(8,128)S(1)}, f32[16,128,128]{2,1,0:T(8,128)S(1)}) fusion(f32[3]{0:T(128)S(1)} %copy-done.15, f32[3,16,128]{2,1,0:T(8,128)S(1)} %bitcast.72, f32[3,16,128]{2,1,0:T(8,128)S(1)} %bitcast.112, ...), kind=kLoop, calls=%fused_computation.10 | loop fusion | flops 14417920 | bytes 5341244 | tf_op jit(solution)/shard_map/reduce_sum | solution.py:55
  24.7 3.1 %fusion.132 = (f32[]{:T(128)}, f32[]{:T(128)}, f32[16,128,128]{2,1,0:T(8,128)S(1)}) fusion(f32[16,128,128]{2,1,0:T(8,128)S(1)} %get-tuple-element.475, f32[16,128]{1,0:T(8,128)S(1)} %bitcast.114, f32[16,128]{1,0:T(8,128)S(1)} %bitcast.138, f32[16,128]{1,0:T(8,128)S(1)} %bitcast.135, f32[16,128]{1,0:T(8,128)S(1)} %bitcast.132, f32[16,128]{1,0:T(8,128)S(1)} %bitcast.123, ...), kind=kLoop, calls=%fused_computation.314 | loop fusion | flops 13107198 | bytes 2162696 | tf_op jit(solution)/shard_map/reduce_sum | solution.py:86
  28.0 7.4 %fusion.160 = (f32[]{:T(128)}, f32[]{:T(128)}, f32[]{:T(128)}, f32[]{:T(128)}, f32[]{:T(128)}, /*index=5*/f32[]{:T(128)}, f32[16,128,128]{2,1,0:T(8,128)S(1)}, f32[16,128,128]{2,1,0:T(8,128)S(1)}, f32[16,128,128]{2,1,0:T(8,128)S(1)}) fusion(f32[16,128,128]{2,1,0:T(8,128)S(1)} %get-tuple-element.471, f32[16,128]{1,0:T(8,128)S(1)} %bitcast.124, ...), kind=kLoop, calls=%fused_computation.342 | loop fusion | flops 39321596 | bytes 6389784 | tf_op jit(solution)/shard_map/reduce_sum | solution.py:86
  35.4 8.2 %multiply_reduce_fusion = (f32[16,128,128]{2,1,0:T(8,128)S(1)}, f32[16,128,128]{2,1,0:T(8,128)S(1)}, f32[3,16,128]{2,1,0:T(8,128)}, f32[3,16,128]{2,1,0:T(8,128)...) fusion(f32[3]{0:T(128)S(1)} %copy-done.11, ...), kind=kLoop, calls=%fused_computation.5 | loop fusion | flops 29061120 | bytes 9756780 | tf_op jit(solution)/shard_map/reduce_sum | solution.py:55
  43.7 7.4 %fusion.146 = (f32[]{:T(128)}, f32[]{:T(128)}, f32[]{:T(128)}, f32[]{:T(128)}, f32[]{:T(128)}, /*index=5*/f32[]{:T(128)}, f32[16,128,128]{2,1,0:T(8,128)S(1)}, f32[16,128,128]{2,1,0:T(8,128)S(1)}, f32[16,128,128]{2,1,0:T(8,128)S(1)}) fusion(f32[16,128,128]{2,1,0:T(8,128)S(1)} %get-tuple-element.470, f32[16,128]{1,0:T(8,128)S(1)} %bitcast.115, ...), kind=kLoop, calls=%fused_computation.328 | loop fusion | flops 39321596 | bytes 6389784 | tf_op jit(solution)/shard_map/reduce_sum | solution.py:86
  51.1 4.8 %rsqrt_multiply_fusion.31 = (f32[16,128,128]{2,1,0:T(8,128)S(1)}, f32[16,128,128]{2,1,0:T(8,128)S(1)}, f32[16,128,128]{2,1,0:T(8,128)S(1)}) fusion(f32[16,128,128]{2,1,0:T(8,128)S(1)} %get-tuple-element.468, f32[16,128]{1,0:T(8,128)S(1)} %bitcast.147, f32[16,128]{1,0:T(8,128)S(1)} %bitcast.144, f32[16,128]{1,0:T(8,128)S(1)} %bitcast.141, ...), kind=kLoop, calls=%fused_computation.241 | loop fusion | flops 27525120 | bytes 6389760 | tf_op jit(solution)/shard_map/mul | solution.py:84
  55.9 10.2 %fusion.4 = (f32[3,16,128]{2,1,0:T(8,128)S(1)}, f32[3,16,128]{2,1,0:T(8,128)S(1)}, f32[16,128,128]{2,1,0:T(8,128)S(1)}, f32[3,16,128]{2,1,0:T(8,128)S(1)}, f32[3...) fusion(f32[16,128,128]{2,1,0:T(8,128)S(1)} %get-tuple-element.5, ...), kind=kLoop, calls=%fused_computation.8 | loop fusion | flops 31383552 | bytes 9879636 | tf_op jit(solution)/shard_map/reduce_sum | solution.py:86
  66.2 4.9 %fusion.167 = (f32[]{:T(128)}, f32[]{:T(128)}, f32[]{:T(128)}, f32[]{:T(128)}, f32[16,128,128]{2,1,0:T(8,128)S(1)}) fusion(f32[16,128,128]{2,1,0:T(8,128)S(1)} %get-tuple-element.459, f32[16,128]{1,0:T(8,128)S(1)} %bitcast.148, f32[16,128]{1,0:T(8,128)S(1)} %bitcast.145, f32[16,128]{1,0:T(8,128)S(1)} %bitcast.142, f32[16,128]{1,0:T(8,128)S(1)} %bitcast.130, ...), kind=kLoop, calls=%fused_computation.349 | loop fusion | flops 23855100 | bytes 4292624 | tf_op jit(solution)/shard_map/reduce_sum | solution.py:86
  71.1 7.0 %fusion.153 = (f32[]{:T(128)}, f32[]{:T(128)}, f32[]{:T(128)}, f32[]{:T(128)}, f32[]{:T(128)}, /*index=5*/f32[]{:T(128)}, f32[16,128,128]{2,1,0:T(8,128)S(1)}, f32[16,128,128]{2,1,0:T(8,128)S(1)}) fusion(f32[16,128,128]{2,1,0:T(8,128)S(1)} %get-tuple-element.460, f32[16,128]{1,0:T(8,128)S(1)} %bitcast.125, f32[16,128]{1,0:T(8,128)S(1)} %bitcast.122, ...), kind=kLoop, calls=%fused_computation.335 | loop fusion | flops 37224444 | bytes 6455320 | tf_op jit(solution)/shard_map/reduce_sum | solution.py:86
  78.1 4.6 %fusion.125 = (f32[]{:T(128)}, f32[]{:T(128)}, f32[]{:T(128)}, f32[]{:T(128)}, f32[16,128,128]{2,1,0:T(8,128)S(1)}) fusion(f32[16,128,128]{2,1,0:T(8,128)S(1)} %get-tuple-element.457, f32[16,128]{1,0:T(8,128)S(1)} %bitcast.192, f32[16,128]{1,0:T(8,128)S(1)} %bitcast.193, f32[16,128]{1,0:T(8,128)S(1)} %bitcast.194, f32[16,128]{1,0:T(8,128)S(1)} %bitcast.191, ...), kind=kLoop, calls=%fused_computation.307 | loop fusion | flops 23855100 | bytes 4292624 | tf_op jit(solution)/shard_map/reduce_sum | solution.py:86
  82.7 3.1 %fusion.22 = (f32[3,16,128]{2,1,0:T(8,128)S(1)}, f32[3,16,128]{2,1,0:T(8,128)S(1)}, f32[3,16,128]{2,1,0:T(8,128)S(1)}, f32[3,16,128]{2,1,0:T(8,128)S(1)}) fusion(f32[16,128,128]{2,1,0:T(8,128)S(1)} %get-tuple-element.497, f32[3,16,128]{2,1,0:T(8,128)S(1)} %bitcast.107, f32[3,16,128]{2,1,0:T(8,128)S(1)} %bitcast.82, f32[16,128,128]{2,1,0:T(8,128)S(1)} %get-tuple-element.505), kind=kLoop, calls=%fused_computation.38 | loop fusion | flops 7053312 | bytes 2244608 | tf_op jit(solution)/shard_map/reduce_sum | solution.py:86
  85.8 0.6 neg.108
  86.8 0.2 scatter-add.119
  87.0 0.8 fusion.319
  87.7 0.8 slice_add_fusion.16
  88.5 0.2 scatter-add.121
  88.8 0.2 scatter-add.125
  89.1 0.2 scatter-add.129
  89.3 5.0 %fusion.10 = (f32[3,16,128]{2,1,0:T(8,128)S(1)}, f32[3,16,128]{2,1,0:T(8,128)S(1)}, f32[3,16,128]{2,1,0:T(8,128)S(1)}, f32[3,16,128]{2,1,0:T(8,128)S(1)}, f32[3,...) fusion(f32[16,128,128]{2,1,0:T(8,128)S(1)} %get-tuple-element.504, f32[3]{0:T(128)S(1)} %copy-done.12, ...), kind=kLoop, calls=%fused_computation.18 | loop fusion | flops 11759616 | bytes 3366948 | tf_op jit(solution)/shard_map/reduce_sum | solution.py:86
  94.5 0.2 scatter-add.135
  94.8 0.2 scatter-add.139
  95.1 0.2 scatter-add.141
  95.4 0.2 scatter-add.145
  95.7 0.2 scatter-add.149
  95.9 3.4 %collective-permute-start.3 = (f32[3,3,5,1,128]{4,3,2,1,0:T(1,128)S(1)}, f32[3,3,5,1,128]{4,3,2,1,0:T(1,128)S(1)}, u32[]{:S(2)}, u32[]{:S(2)}) collective-permute-start(f32[3,3,5,1,128]{4,3,2,1,0:T(1,128)S(1)} %slice.1705), channel_id=1, source_target_pairs={{0,1},{1,2},{2,3},{3,4},{4,5},{5,6},{6,7},{7,8},{8,9},{9,10},{10,1... | collective-permute-start | bytes 69128 | tf_op jit(solution)/shard_map/ppermute | solution.py:26
  99.4 12.6 %collective-permute-done.3 = f32[3,3,5,1,128]{4,3,2,1,0:T(1,128)S(1)} collective-permute-done((f32[3,3,5,1,128]{4,3,2,1,0:T(1,128)S(1)}, f32[3,3,5,1,128]{4,3,2,1,0:T(1,128)S(1)}, u32[]{:S(2)}, u32[]{:S(2)}) %collective-permute-start.3) | collective-permute-done | bytes 23072 | tf_op jit(solution)/shard_map/ppermute | solution.py:26
  112.0 0.1 scatter-add.150
  112.2 2.0 %collective-permute-start.4 = (f32[3,3,1,2,128]{4,3,2,1,0:T(2,128)S(1)}, f32[3,3,1,2,128]{4,3,2,1,0:T(2,128)S(1)}, u32[]{:S(2)}, u32[]{:S(2)}) collective-permute-start(f32[3,3,1,2,128]{4,3,2,1,0:T(2,128)S(1)} %slice.1708), channel_id=1, source_target_pairs={{0,12},{12,24},{24,36},{36,48},{48,60},{60,72},{72,84},{84,0},{1,1... | collective-permute-start | bytes 27656 | tf_op jit(solution)/shard_map/ppermute | solution.py:26
  131.8 18.2 %all-reduce.1 = (f32[]{:T(128)}, f32[]{:T(128)}) all-reduce(f32[]{:T(128)S(6)} %add.1007, f32[]{:T(128)S(6)} %add.994), channel_id=1, replica_groups=mesh['gx'=8,'gy_0'=4,'gy_1'=2,'gz_0'=3,'gz_1'=4] {'gx'}, use_global_device_ids=true, to_apply=%region_78.0 | all-reduce | flops 2 | bytes 16 | tf_op jit(solution)/shard_map/psum | solution.py:30
  150.0 13.7 %all-reduce.3 = (f32[]{:T(128)}, f32[]{:T(128)}) all-reduce(f32[]{:T(128)} %get-tuple-element.485, f32[]{:T(128)} %get-tuple-element.486), channel_id=1, replica_groups=mesh['gx'=8,'gy_0'=4,'gy_1'=2,'gz_0'=3,'gz_1'=4] {'gy_0'}, use_global_device_ids=true, to_apply=%region_79.0 | all-reduce | flops 2 | bytes 16 | tf_op jit(solution)/shard_map/psum | solution.py:30
  163.7 3.1 %all-reduce.5 = (f32[]{:T(128)}, f32[]{:T(128)}) all-reduce(f32[]{:T(128)} %get-tuple-element.489, f32[]{:T(128)} %get-tuple-element.490), channel_id=1, replica_groups=mesh['gx'=8,'gy_0'=4,'gy_1'=2,'gz_0'=3,'gz_1'=4] {'gy_1'}, use_global_device_ids=true, to_apply=%region_80.0 | all-reduce | flops 2 | bytes 16 | tf_op jit(solution)/shard_map/psum | solution.py:30
  166.8 9.4 %all-reduce.4 = (f32[]{:T(128)}, f32[]{:T(128)}) all-reduce(f32[]{:T(128)} %get-tuple-element.493, f32[]{:T(128)} %get-tuple-element.494), channel_id=1, replica_groups=mesh['gx'=8,'gy_0'=4,'gy_1'=2,'gz_0'=3,'gz_1'=4] {'gz_0'}, use_global_device_ids=true, to_apply=%region_81.0 | all-reduce | flops 2 | bytes 16 | tf_op jit(solution)/shard_map/psum | solution.py:30
  176.3 16.9 %all-reduce.2 = (f32[1]{0:T(128)}, f32[1]{0:T(128)}) all-reduce(f32[1]{0:T(128)} %bitcast.71, f32[1]{0:T(128)} %bitcast.70), channel_id=1, replica_groups=mesh['gx'=8,'gy_0'=4,'gy_1'=2,'gz_0'=3,'gz_1'=4] {'gz_1'}, use_global_device_ids=true, to_apply=%region_82.0 | all-reduce | flops 2 | bytes 16 | tf_op jit(solution)/shard_map/psum | solution.py:30
  193.2 1.9 collective-permute-start.5
  195.1 1.9 maximum_multiply_fusion
  197.0 2.9 %collective-permute-done.5 = f32[3,1,4,2,128]{4,3,2,1,0:T(2,128)S(1)} collective-permute-done((f32[3,1,4,2,128]{4,3,2,1,0:T(2,128)S(1)}, f32[3,1,4,2,128]{4,3,2,1,0:T(2,128)S(1)}, u32[]{:S(2)}, u32[]{:S(2)}) %collective-permute-start.5) | collective-permute-done | bytes 12320 | tf_op jit(solution)/shard_map/ppermute | solution.py:26
  200.0 0.6 copy-done.3
  (104 shorter events, 1.7 us)
Async XLA Ops:
  0.6 20.6 %copy-start.5 = (f32[3]{0:T(128)S(1)}, f32[3]{0:T(128)}, u32[]{:S(2)}) copy-start(f32[3]{0:T(128)} %constant.879.clone) | copy-start | bytes 40
  0.6 20.6 %copy-start.13 = (f32[3]{0:T(128)S(1)}, f32[3]{0:T(128)}, u32[]{:S(2)}) copy-start(f32[3]{0:T(128)} %constant.880.clone) | copy-start | bytes 40
  0.7 20.6 %copy-start.14 = (f32[3]{0:T(128)S(1)}, f32[3]{0:T(128)}, u32[]{:S(2)}) copy-start(f32[3]{0:T(128)} %constant.883.clone) | copy-start | bytes 40
  0.7 20.5 %copy-start.6 = (f32[3]{0:T(128)S(1)}, f32[3]{0:T(128)}, u32[]{:S(2)}) copy-start(f32[3]{0:T(128)} %constant.886.clone) | copy-start | bytes 40
  0.7 20.5 %copy-start.15 = (f32[3]{0:T(128)S(1)}, f32[3]{0:T(128)}, u32[]{:S(2)}) copy-start(f32[3]{0:T(128)} %constant.890.clone) | copy-start | bytes 40
  0.7 20.5 %copy-start = (f32[3,2,4,2,128]{4,3,2,1,0:T(2,128)S(1)}, f32[3,2,4,2,128]{4,3,2,1,0:T(2,128)}, u32[]{:S(2)}) copy-start(f32[3,2,4,2,128]{4,3,2,1,0:T(2,128)} %param.82) | copy-start | bytes 73732
  4.5 6.9 %collective-permute-start = (f32[7,1,4,2,128]{4,3,2,1,0:T(2,128)S(1)}, f32[7,1,4,2,128]{4,3,2,1,0:T(2,128)S(1)}, u32[]{:S(2)}, u32[]{:S(2)}) collective-permute-start(f32[7,1,4,2,128]{4,3,2,1,0:T(2,128)S(1)} %slice.1661), channel_id=1, source_target_pairs={{0,672},{96,0},{192,96},{288,192},{384,288},{480,384},{576,480},{6... | collective-permute-start | bytes 86024 | tf_op jit(solution)/shard_map/ppermute | solution.py:26
  11.4 3.4 %collective-permute-start.1 = (f32[7,3,1,2,128]{4,3,2,1,0:T(2,128)S(1)}, f32[7,3,1,2,128]{4,3,2,1,0:T(2,128)S(1)}, u32[]{:S(2)}, u32[]{:S(2)}) collective-permute-start(f32[7,3,1,2,128]{4,3,2,1,0:T(2,128)S(1)} %pad_maximum_fusion.3), channel_id=1, source_target_pairs={{0,84},{12,0},{24,12},{36,24},{48,36},{60,48},{72,60},{84,72},{1,8... | collective-permute-start | bytes 64520 | tf_op jit(solution)/shard_map/ppermute | solution.py:26
  15.0 6.0 %collective-permute-start.2 = (f32[7,3,5,1,128]{4,3,2,1,0:T(1,128)S(1)}, f32[7,3,5,1,128]{4,3,2,1,0:T(1,128)S(1)}, u32[]{:S(2)}, u32[]{:S(2)}) collective-permute-start(f32[7,3,5,1,128]{4,3,2,1,0:T(1,128)S(1)} %slice.1680), channel_id=1, source_target_pairs={{0,11},{1,0},{2,1},{3,2},{4,3},{5,4},{6,5},{7,6},{8,7},{9,8},{10,9... | collective-permute-start | bytes 161288 | tf_op jit(solution)/shard_map/ppermute | solution.py:26
  27.9 7.5 %copy-start.7 = (f32[3]{0:T(128)S(1)}, f32[3]{0:T(128)}, u32[]{:S(2)}) copy-start(f32[3]{0:T(128)} %constant.881.clone) | copy-start | bytes 40
  27.9 7.5 %copy-start.8 = (f32[3]{0:T(128)S(1)}, f32[3]{0:T(128)}, u32[]{:S(2)}) copy-start(f32[3]{0:T(128)} %constant.882.clone) | copy-start | bytes 40
  27.9 7.5 %copy-start.9 = (f32[3]{0:T(128)S(1)}, f32[3]{0:T(128)}, u32[]{:S(2)}) copy-start(f32[3]{0:T(128)} %constant.884.clone) | copy-start | bytes 40
  27.9 7.4 %copy-start.10 = (f32[3]{0:T(128)S(1)}, f32[3]{0:T(128)}, u32[]{:S(2)}) copy-start(f32[3]{0:T(128)} %constant.888.clone) | copy-start | bytes 40
  27.9 7.4 %copy-start.11 = (f32[3]{0:T(128)S(1)}, f32[3]{0:T(128)}, u32[]{:S(2)}) copy-start(f32[3]{0:T(128)} %constant.891.clone) | copy-start | bytes 40
  28.0 7.4 %copy-start.12 = (f32[3]{0:T(128)S(1)}, f32[3]{0:T(128)}, u32[]{:S(2)}) copy-start(f32[3]{0:T(128)} %constant.889.clone) | copy-start | bytes 40
  51.1 4.8 %copy-start.4 = (f32[3]{0:T(128)S(1)}, f32[3]{0:T(128)}, u32[]{:S(2)}) copy-start(f32[3]{0:T(128)} %constant.887.clone) | copy-start | bytes 40
  89.3 6.0 %copy-start.1 = (f32[3,16,128]{2,1,0:T(8,128)S(1)}, f32[3,16,128]{2,1,0:T(8,128)}, u32[]{:S(2)}) copy-start(f32[3,16,128]{2,1,0:T(8,128)} %get-tuple-element.462) | copy-start | bytes 73732
  89.3 6.0 %copy-start.2 = (f32[3,16,128]{2,1,0:T(8,128)S(1)}, f32[3,16,128]{2,1,0:T(8,128)}, u32[]{:S(2)}) copy-start(f32[3,16,128]{2,1,0:T(8,128)} %get-tuple-element.461) | copy-start | bytes 73732
  95.9 16.0 %collective-permute-start.3 = (f32[3,3,5,1,128]{4,3,2,1,0:T(1,128)S(1)}, f32[3,3,5,1,128]{4,3,2,1,0:T(1,128)S(1)}, u32[]{:S(2)}, u32[]{:S(2)}) collective-permute-start(f32[3,3,5,1,128]{4,3,2,1,0:T(1,128)S(1)} %slice.1705), channel_id=1, source_target_pairs={{0,1},{1,2},{2,3},{3,4},{4,5},{5,6},{6,7},{7,8},{8,9},{9,10},{10,1... | collective-permute-start | bytes 69128 | tf_op jit(solution)/shard_map/ppermute | solution.py:26
  112.2 81.0 %collective-permute-start.4 = (f32[3,3,1,2,128]{4,3,2,1,0:T(2,128)S(1)}, f32[3,3,1,2,128]{4,3,2,1,0:T(2,128)S(1)}, u32[]{:S(2)}, u32[]{:S(2)}) collective-permute-start(f32[3,3,1,2,128]{4,3,2,1,0:T(2,128)S(1)} %slice.1708), channel_id=1, source_target_pairs={{0,12},{12,24},{24,36},{36,48},{48,60},{60,72},{72,84},{84,0},{1,1... | collective-permute-start | bytes 27656 | tf_op jit(solution)/shard_map/ppermute | solution.py:26
  193.2 6.8 %collective-permute-start.5 = (f32[3,1,4,2,128]{4,3,2,1,0:T(2,128)S(1)}, f32[3,1,4,2,128]{4,3,2,1,0:T(2,128)S(1)}, u32[]{:S(2)}, u32[]{:S(2)}) collective-permute-start(f32[3,1,4,2,128]{4,3,2,1,0:T(2,128)S(1)} %slice.1711), channel_id=1, source_target_pairs={{0,96},{96,192},{192,288},{288,384},{384,480},{480,576},{576,672},... | collective-permute-start | bytes 36872 | tf_op jit(solution)/shard_map/ppermute | solution.py:26
  200.0 0.6 copy-start.3
where the time goes:
time: 202 us; the launch traced here: 201 us
  other arithmetic  75.3 us (37%)
  blocking collectives  61.3 us (30%)
  waiting for transfers between devices  21.9 us (11%)
  between operations  19.1 us (9%)
  starting transfers between devices  17.1 us (8%)
  local copies, waits for them, and re-layouts  5.94 us (3%)
    psum x5, blocking collectives, one_axis_at_a_time(): return functools.reduce(lax.psum, axes, value)  61.3 us
    reduce_sum x6, other arithmetic, pair_terms(): jnp.sum(energy)  34.4 us
    ppermute x6, waiting for transfers between devices, passed_along(): return lax.ppermute(value, axis, pairs)  21.9 us
    reduce_sum x3, other arithmetic, pair_terms(): jnp.sum(weighted, 2)  18.3 us
    ppermute x6, starting transfers between devices, passed_along(): return lax.ppermute(value, axis, pairs)  17.1 us
    reduce_sum x2, other arithmetic, pair_terms(): dist_sq = jnp.sum(displace * displace, 0)  11.7 us
    mul x1, other arithmetic, pair_terms(): slope = live_mask * (slope_here - slope_cut) * inverse  4.8 us
  transfers between devices with their start and end apart: 6, of which 5 were waited for; matrix products, arithmetic and copies ran while one was open for 1% of the time, Pallas kernels for 0%

commit v1 on v0

v1 whole, which is shorter than its diff:
```python
import functools

import jax
import jax.numpy as jnp
from jax import lax
from jax.experimental import pallas as pl
from jax.experimental.pallas import tpu as pltpu
from jax.sharding import Mesh
from jax.sharding import PartitionSpec as P

GY = ("gy_0", "gy_1")
GZ = ("gz_0", "gz_1")
GX_GY_GZ = ("gx", "gy_0", "gy_1", "gz_0", "gz_1")

soft_core = 0.09
cut_sq = 1.0 + soft_core
far_away = 2.0
corner_pairs = [
    (first_corner, second_corner)
    for first_corner in range(8)
    for second_corner in range(8)
    if first_corner & second_corner == 0 and first_corner <= second_corner
]


def corner_of(which):
    return (which & 1, which >> 1 & 1, which >> 2 & 1)


def passed_along(value, axis, steps):
    count = lax.axis_size(axis)
    pairs = [(source, (source + steps) % count) for source in range(count)]
    return lax.ppermute(value, axis, pairs)


def one_axis_at_a_time(value, axes):
    return functools.reduce(lax.psum, axes, value)


def fill_tables(param_ref, table_ref):
    tile = (8, 128)
    charge = [jnp.full(tile, param_ref[0, kind], jnp.float32) for kind in range(2)]
    sigma = [jnp.full(tile, param_ref[1, kind], jnp.float32) for kind in range(2)]
    root = [jnp.sqrt(jnp.full(tile, param_ref[2, kind], jnp.float32)) for kind in range(2)]
    for first in range(2):
        for second in range(2):
            width = 0.5 * (sigma[first] + sigma[second])
            width_six = (width * width) * (width * width) * (width * width)
            attract = 24.0 * (root[first] * root[second]) * width_six
            repel = attract * width_six
            coulomb = charge[first] * charge[second]
            parts, inverse, square = pair_parts(jnp.full(tile, cut_sq, jnp.float32), attract, repel, coulomb)
            lennard, charged, steep = parts
            value = lennard * (1.0 / 6.0) + charged
            level = -(value + (square * inverse) * steep)
            for at, entry in enumerate((attract, repel, coulomb, steep, level)):
                table_ref[(first * 2 + second) * 5 + at] = entry


def pair_parts(square, attract, repel, coulomb):
    inverse = lax.rsqrt(square)
    two = inverse * inverse
    six = (two * two) * two
    pulled = attract * six
    pushed = repel * (six * six)
    lennard = pushed - pulled
    charged = coulomb * inverse
    steep = ((lennard + pushed) + charged) * inverse
    return (lennard, charged, steep), inverse, square


def fill_cell(cell_ref, column_ref, row_ref, kind_ref, cell, place, as_first):
    atoms = cell_ref[cell]
    row = lax.broadcasted_iota(jnp.int32, (8, 128), 0)
    shift = jnp.where(row == 0, place[0], jnp.where(row == 1, place[1], place[2]))
    spot = jnp.where(row < 3, atoms + shift, 0.0)
    norm = jnp.sum(spot * spot, 0, keepdims=True) + 0.5 * soft_core + far_away * (1.0 - atoms[4:5])
    whole = jnp.where(row == 3, jnp.broadcast_to(norm, (8, 128)), spot)
    high = whole.astype(jnp.bfloat16).astype(jnp.float32)
    middle = (whole - high).astype(jnp.bfloat16).astype(jnp.float32)
    low = ((whole - high) - middle).astype(jnp.bfloat16).astype(jnp.float32)

    def down(value, by):
        return pltpu.roll(value, by, 0)

    xyz = row < 3
    xyz_down = (row > 3) & (row < 7)
    middle_down = jnp.where(xyz_down, down(middle, 4), 0.0)
    rows = [
        jnp.where(xyz, high, jnp.where(xyz_down, middle_down, 1.0)),
        jnp.where(
            xyz,
            low,
            jnp.where(
                row == 3,
                1.0,
                jnp.where(
                    row == 4,
                    down(high, 1),
                    jnp.where(row == 5, down(middle, 2), jnp.where(row == 6, down(low, 3), 0.0)),
                ),
            ),
        ),
        jnp.where(xyz, high, middle_down),
        jnp.where(xyz, high, 0.0),
    ]
    row_ref[cell] = jnp.concatenate(rows, 0).astype(jnp.bfloat16)
    if not as_first:
        return
    high_two = -2.0 * high
    middle_two = -2.0 * middle
    columns = [
        jnp.where(
            row < 4,
            jnp.where(xyz, high_two, high),
            down(jnp.where(xyz, high_two, middle), 4),
        ),
        jnp.where(xyz, high_two, jnp.where(row == 3, low, jnp.where(row == 7, 0.0, 1.0))),
        jnp.where(xyz, middle_two, jnp.where(xyz_down, down(middle_two, 4), 0.0)),
        jnp.where(xyz, -2.0 * low, 0.0),
    ]
    stacked = jnp.concatenate(columns + [jnp.zeros((96, 128), jnp.float32)], 0)
    column_ref[cell] = jnp.transpose(stacked)[:, :32].astype(jnp.bfloat16)
    kind_ref[cell] = jnp.transpose(jnp.broadcast_to(atoms[3:4], (128, 128)))


def pair_kernel(sizes, param_ref, cell_ref, force_ref, total_ref, column_ref, row_ref, kind_ref, table_ref, sum_ref):
    size_x, size_y, size_z = sizes
    wide_y, wide_z = size_y + 1, size_z + 1
    cells = (size_x + 1) * wide_y * wide_z
    fill_tables(param_ref, table_ref)

    def middle_of(cell):
        at = (cell // (wide_y * wide_z), cell // wide_z % wide_y, cell % wide_z)
        return [float(a) - (size + 1) / 2 for a, size in zip(at, sizes)]

    for cell in range(cells):
        fill_cell(cell_ref, column_ref, row_ref, kind_ref, cell, middle_of(cell), cell % wide_z < size_z)
    sum_ref[...] = jnp.zeros_like(sum_ref)
    tile = (8, 128)

    def block(first, second, selfpair, energy):
        square = lax.dot_general(
            column_ref[first], row_ref[second], (((1,), (0,)), ((), ())), preferred_element_type=jnp.float32
        )
        kind_second = jnp.broadcast_to(cell_ref[second, 3:4], tile) > 0.5
        rows = [
            [
                jnp.where(kind_second, table_ref[(kind * 2 + 1) * 5 + at], table_ref[kind * 2 * 5 + at])
                for at in range(5)
            ]
            for kind in range(2)
        ]
        highs, lows = [], []
        partial = jnp.zeros(tile, jnp.float32)
        for pack in range(8):
            slopes = []
            for half in range(2):
                at = pack * 16 + half * 8
                kind_first = kind_ref[first, at : at + 8, :] > 0.5
                attract, repel, coulomb, steep_cut, level = (
                    jnp.where(kind_first, one, zero) for zero, one in zip(*rows)
                )
                here = square[at : at + 8]
                if selfpair:
                    lane = lax.broadcasted_iota(jnp.int32, tile, 1)
                    sublane = lax.broadcasted_iota(jnp.int32, tile, 0)
                    here = jnp.where(lane == sublane + at, cut_sq, here)
                (lennard, charged, steep), inverse, here = pair_parts(
                    jnp.minimum(here, cut_sq), attract, repel, coulomb
                )
                value = lennard * (1.0 / 6.0) + charged
                partial = partial + ((value + (here * inverse) * steep_cut) + level)
                slopes.append((steep - steep_cut) * inverse)
            slope = jnp.concatenate(slopes, 0)
            high = slope.astype(jnp.bfloat16)
            highs.append(high)
            lows.append((slope - high.astype(jnp.float32)).astype(jnp.bfloat16))
        high = jnp.concatenate(highs, 0)
        low = jnp.concatenate(lows, 0)
        across = (((1,), (1,)), ((), ()))
        along = (((1,), (0,)), ((), ()))
        dot = functools.partial(lax.dot_general, preferred_element_type=jnp.float32)
        of_second = row_ref[second, 0:16, :]
        on_first = dot(of_second, high, across) + dot(of_second, low, across)
        if selfpair:
            return on_first, None, energy + 0.5 * partial
        of_first = row_ref[first, 0:16, :]
        on_second = dot(of_first, high, along) + dot(of_first, low, along)
        return on_first, on_second, energy + partial

    def one_cell(member, energy):
        base = (
            member // (size_y * size_z) * (wide_y * wide_z)
            + member // size_z % size_y * wide_z
            + member % size_z
        )
        for first_corner, second_corner in corner_pairs:
            first, second = (
                base + x * (wide_y * wide_z) + y * wide_z + z
                for x, y, z in (corner_of(first_corner), corner_of(second_corner))
            )
            on_first, on_second, energy = block(first, second, first_corner == second_corner, energy)
            sum_ref[first] = sum_ref[first] + on_first
            if on_second is not None:
                sum_ref[second] = sum_ref[second] + on_second
        return energy

    energy = lax.fori_loop(0, size_x * size_y * size_z, one_cell, jnp.zeros(tile, jnp.float32))
    total_ref[0] = energy
    virial = jnp.zeros((1, 128), jnp.float32)
    row = lax.broadcasted_iota(jnp.int32, tile, 0)
    for cell in range(cells):
        place = middle_of(cell)
        shift = jnp.where(row == 0, place[0], jnp.where(row == 1, place[1], place[2]))
        spot = jnp.where(row < 3, cell_ref[cell] + shift, 0.0)
        upper, lower = sum_ref[cell, 0:8, :], sum_ref[cell, 8:16, :]
        moved = jnp.where(row < 3, upper + pltpu.roll(upper, 4, 0) + lower, 0.0)
        slopes = upper[3:4]
        norm = (
            jnp.sum(spot * spot, 0, keepdims=True)
            + (0.5 * soft_core - soft_core)
            + far_away * (1.0 - cell_ref[cell, 4:5])
        )
        crossed = lower[4:5] + lower[5:6] + lower[6:7]
        virial = virial + (norm * slopes + crossed - 2.0 * jnp.sum(spot * moved, 0, keepdims=True))
        force_ref[cell] = spot * slopes - moved
    total_ref[1] = jnp.where(row == 0, jnp.broadcast_to(-0.5 * virial, tile), 0.0)


def pair_sums(params, atoms, sizes):
    cells = atoms.shape[0]
    return pl.pallas_call(
        functools.partial(pair_kernel, sizes),
        out_shape=(
            jax.ShapeDtypeStruct((cells, 8, 128), jnp.float32),
            jax.ShapeDtypeStruct((2, 8, 128), jnp.float32),
        ),
        in_specs=[
            pl.BlockSpec(memory_space=pltpu.SMEM),
            pl.BlockSpec(memory_space=pltpu.VMEM),
        ],
        out_specs=(
            pl.BlockSpec(memory_space=pltpu.VMEM),
            pl.BlockSpec(memory_space=pltpu.VMEM),
        ),
        scratch_shapes=[
            pltpu.VMEM((cells, 128, 32), jnp.bfloat16),
            pltpu.VMEM((cells, 32, 128), jnp.bfloat16),
            pltpu.VMEM((cells, 128, 128), jnp.float32),
            pltpu.VMEM((20, 8, 128), jnp.float32),
            pltpu.VMEM((cells, 16, 128), jnp.float32),
        ],
        name="pair_sums",
    )(params, atoms)


def per_device(positions, type_ids, counts, type_charge, type_sigma, type_epsilon):
    size_x, size_y, size_z, width_atoms = positions.shape[1:]
    slots = lax.broadcasted_iota(jnp.int32, type_ids.shape, 3)
    occupied = (slots < counts[..., None]).astype(jnp.float32)
    blank = jnp.zeros(type_ids.shape, jnp.float32)
    atoms = jnp.stack(
        [positions[0], positions[1], positions[2], type_ids.astype(jnp.float32), occupied, blank, blank, blank], 3
    )
    extended = jnp.concatenate([atoms, passed_along(atoms[:1], "gx", -1)], 0)
    extended = jnp.concatenate([extended, passed_along(extended[:, :1], GY, -1)], 1)
    extended = jnp.concatenate([extended, passed_along(extended[:, :, :1], GZ, -1)], 2)
    wide = extended.shape[:3]
    params = jnp.stack([type_charge, type_sigma, type_epsilon])
    forces, sums = pair_sums(
        params, extended.reshape((-1, 8, width_atoms)), (size_x, size_y, size_z)
    )
    reaction = forces.reshape(wide + (8, width_atoms))[..., :3, :]
    returned = passed_along(reaction[:, :, size_z:], GZ, 1)
    reaction = reaction[:, :, :size_z].at[:, :, :1].add(returned)
    returned = passed_along(reaction[:, size_y:], GY, 1)
    reaction = reaction[:, :size_y].at[:, :1].add(returned)
    returned = passed_along(reaction[size_x:], "gx", 1)
    forces = reaction[:size_x].at[:1].add(returned)
    summed = one_axis_at_a_time(jnp.sum(sums, (1, 2)), GX_GY_GZ)
    normaliser = 1.0 / (
        size_x
        * lax.axis_size("gx")
        * size_y
        * lax.axis_size(GY)
        * size_z
        * lax.axis_size(GZ)
        * width_atoms
    )
    return (jnp.transpose(forces, (3, 0, 1, 2, 4)), summed * normaliser)


def solution(mesh):
    split = Mesh(
        mesh.devices.reshape(mesh.shape["gx"], 4, 2, 3, 4), ("gx", "gy_0", "gy_1", "gz_0", "gz_1")
    )
    placed = (P(None, "gx", GY, GZ, None), P("gx", GY, GZ, None), P("gx", GY, GZ), P(), P(), P())
    return jax.shard_map(
        per_device,
        mesh=split,
        in_specs=placed,
        out_specs=(P(None, "gx", GY, GZ, None), P()),
        check_vma=False,
    )
```

time: 202 us -> 159 us (0.79)
  the two profiles are of different devices: /device:TPU:66 before, /device:TPU:2 now
where the time goes in v1:
time: 159 us
  Pallas kernels  53.9 us (34%)
  blocking collectives  53.5 us (34%)
  starting transfers between devices  23.3 us (15%)
  waiting for transfers between devices  20.9 us (13%)
  local copies, waits for them, and re-layouts  4.16 us (3%)
  other arithmetic  2.04 us (1%)
    pallas_call x1, Pallas kernels, pair_sums(): pl.pallas_call(functools.partial(pair_kernel, sizes), out_shape=(jax.Shap...  53.9 us
    psum x5, blocking collectives, one_axis_at_a_time(): return functools.reduce(lax.psum, axes, value)  53.5 us
    ppermute x6, starting transfers between devices, passed_along(): return lax.ppermute(value, axis, pairs)  23.3 us
    ppermute x6, waiting for transfers between devices, passed_along(): return lax.ppermute(value, axis, pairs)  20.9 us
  transfers between devices with their start and end apart: 6, of which 5 were waited for; matrix products, arithmetic and copies ran while one was open for 1% of the time, Pallas kernels for 0%

profile of v1, /device:TPU:2, one launch (start us, length us, event | category | flops | bytes accessed | tf_op | source)
XLA Modules:
  0.0 158.7 jit_solution(4027459554603848109)
XLA Ops:
  0.6 0.0 copy-start.3
  0.6 0.0 copy-start
  0.6 0.8 copy.8
  1.4 0.1 compare_convert_fusion
  1.5 0.0 copy-done.3
  1.5 0.0 copy-done
  1.6 0.1 stack.28
  1.7 5.4 %collective-permute-start = (f32[1,4,2,8,128]{4,3,2,1,0:T(8,128)S(1)}, f32[1,4,2,8,128]{4,3,2,1,0:T(8,128)S(1)}, u32[]{:S(2)}, u32[]{:S(2)}) collective-permute-start(f32[1,4,2,8,128]{4,3,2,1,0:T(8,128)S(1)} %slice.159), channel_id=1, source_target_pairs={{0,672},{96,0},{192,96},{288,192},{384,288},{480,384},{576,480},{6... | collective-permute-start | bytes 98312 | tf_op jit(solution)/shard_map/ppermute | solution.py:33
  7.1 1.6 collective-permute-done
  8.7 6.5 %collective-permute-start.1 = (f32[3,1,2,8,128]{4,3,2,1,0:T(8,128)S(1)}, f32[3,1,2,8,128]{4,3,2,1,0:T(8,128)S(1)}, u32[]{:S(2)}, u32[]{:S(2)}) collective-permute-start(f32[3,1,2,8,128]{4,3,2,1,0:T(8,128)S(1)} %pad_maximum_fusion.3), channel_id=1, source_target_pairs={{0,84},{12,0},{24,12},{36,24},{48,36},{60,48},{72,60},{84,72},{1,8... | collective-permute-start | bytes 73736 | tf_op jit(solution)/shard_map/ppermute | solution.py:33
  15.2 1.5 collective-permute-done.1
  16.7 5.7 %collective-permute-start.2 = (f32[3,5,1,8,128]{4,3,2,1,0:T(8,128)S(1)}, f32[3,5,1,8,128]{4,3,2,1,0:T(8,128)S(1)}, u32[]{:S(2)}, u32[]{:S(2)}) collective-permute-start(f32[3,5,1,8,128]{4,3,2,1,0:T(8,128)S(1)} %pad_maximum_fusion.1), channel_id=1, source_target_pairs={{0,11},{1,0},{2,1},{3,2},{4,3},{5,4},{6,5},{7,6},{8,7},{9,8},{10,9... | collective-permute-start | bytes 184328 | tf_op jit(solution)/shard_map/ppermute | solution.py:33
  22.4 0.0 copy-start.4
  22.4 0.0 copy-start.5
  22.4 0.0 copy-start.6
  22.4 0.6 copy-done.4
  23.0 0.0 copy-done.5
  23.0 0.0 copy-done.6
  23.1 0.6 pad_maximum_fusion.4.param_ref
  23.6 0.6 collective-permute-done.2
  24.2 0.7 pad_maximum_fusion
  24.9 53.9 %pair_sums.1 = (f32[45,8,128]{2,1,0:T(8,128)}, f32[2,8,128]{2,1,0:T(8,128)}) custom-call(f32[3,2]{1,0:T(4,128)} %pad_maximum_fusion.4.param_ref, f32[45,8,128]{2,1,0:T(8,128)} %bitcast.18), custom_call_target="tpu_custom_call" | custom-call | tf_op jit(solution)/shard_map/pair_sums/pallas_call | solution.py:233
  78.8 0.9 fusion.2
  79.7 2.0 %collective-permute-start.3 = (f32[3,5,1,3,128]{4,2,1,0,3:T(1,128)S(1)}, f32[3,5,1,3,128]{4,2,1,0,3:T(1,128)S(1)}, u32[]{:S(2)}, u32[]{:S(2)}) collective-permute-start(f32[3,5,1,3,128]{4,2,1,0,3:T(1,128)S(1)} %copy.18), channel_id=1, source_target_pairs={{0,1},{1,2},{2,3},{3,4},{4,5},{5,6},{6,7},{7,8},{8,9},{9,10},{10,1... | collective-permute-start | bytes 69128 | tf_op jit(solution)/shard_map/ppermute | solution.py:33
  81.6 0.9 slice.160
  82.6 12.9 %collective-permute-done.3 = f32[3,5,1,3,128]{4,2,1,0,3:T(1,128)S(1)} collective-permute-done((f32[3,5,1,3,128]{4,2,1,0,3:T(1,128)S(1)}, f32[3,5,1,3,128]{4,2,1,0,3:T(1,128)S(1)}, u32[]{:S(2)}, u32[]{:S(2)}) %collective-permute-start.3) | collective-permute-done | bytes 23072 | tf_op jit(solution)/shard_map/ppermute | solution.py:33
  95.5 0.1 scatter-add.10
  95.6 0.0 copy-start.2
  95.7 1.9 %collective-permute-start.4 = (f32[3,1,2,3,128]{4,2,1,0,3:T(2,128)S(1)}, f32[3,1,2,3,128]{4,2,1,0,3:T(2,128)S(1)}, u32[]{:S(2)}, u32[]{:S(2)}) collective-permute-start(f32[3,1,2,3,128]{4,2,1,0,3:T(2,128)S(1)} %slice.165), channel_id=1, source_target_pairs={{0,12},{12,24},{24,36},{36,48},{48,60},{60,72},{72,84},{84,0},{1,1... | collective-permute-start | bytes 27656 | tf_op jit(solution)/shard_map/ppermute | solution.py:33
  97.6 0.0 copy-done.2
  97.6 0.1 reduce_sum.9
  97.7 17.7 %psum.35 = f32[2]{0:T(128)S(1)} all-reduce(f32[2]{0:T(128)S(1)} %reduce_sum.9), channel_id=1, replica_groups=mesh['gx'=8,'gy_0'=4,'gy_1'=2,'gz_0'=3,'gz_1'=4] {'gx'}, use_global_device_ids=true, to_apply=%region_1.0 | all-reduce | flops 2 | bytes 16 | tf_op jit(solution)/shard_map/psum | solution.py:37
  115.4 8.4 %psum.36 = f32[2]{0:T(128)S(1)} all-reduce(f32[2]{0:T(128)S(1)} %psum.35), channel_id=1, replica_groups=mesh['gx'=8,'gy_0'=4,'gy_1'=2,'gz_0'=3,'gz_1'=4] {'gy_0'}, use_global_device_ids=true, to_apply=%region_2.0 | all-reduce | flops 2 | bytes 16 | tf_op jit(solution)/shard_map/psum | solution.py:37
  123.8 2.5 %psum.37 = f32[2]{0:T(128)S(1)} all-reduce(f32[2]{0:T(128)S(1)} %psum.36), channel_id=1, replica_groups=mesh['gx'=8,'gy_0'=4,'gy_1'=2,'gz_0'=3,'gz_1'=4] {'gy_1'}, use_global_device_ids=true, to_apply=%region_3.0 | all-reduce | flops 2 | bytes 16 | tf_op jit(solution)/shard_map/psum | solution.py:37
  126.2 8.8 %psum.38 = f32[2]{0:T(128)S(1)} all-reduce(f32[2]{0:T(128)S(1)} %psum.37), channel_id=1, replica_groups=mesh['gx'=8,'gy_0'=4,'gy_1'=2,'gz_0'=3,'gz_1'=4] {'gz_0'}, use_global_device_ids=true, to_apply=%region_4.0 | all-reduce | flops 2 | bytes 16 | tf_op jit(solution)/shard_map/psum | solution.py:37
  135.1 16.2 %psum.39 = f32[2]{0:T(128)S(1)} all-reduce(f32[2]{0:T(128)S(1)} %psum.38), channel_id=1, replica_groups=mesh['gx'=8,'gy_0'=4,'gy_1'=2,'gz_0'=3,'gz_1'=4] {'gz_1'}, use_global_device_ids=true, to_apply=%region_5.0 | all-reduce | flops 2 | bytes 16 | tf_op jit(solution)/shard_map/psum | solution.py:37
  151.2 0.0 collective-permute-done.4
  151.3 1.9 %collective-permute-start.5 = (f32[1,4,2,3,128]{4,2,1,0,3:T(2,128)S(1)}, f32[1,4,2,3,128]{4,2,1,0,3:T(2,128)S(1)}, u32[]{:S(2)}, u32[]{:S(2)}) collective-permute-start(f32[1,4,2,3,128]{4,2,1,0,3:T(2,128)S(1)} %slice.168), channel_id=1, source_target_pairs={{0,96},{96,192},{192,288},{288,384},{384,480},{480,576},{576,672},... | collective-permute-start | bytes 36872 | tf_op jit(solution)/shard_map/ppermute | solution.py:33
  153.2 0.5 broadcast_multiply_fusion
  153.7 4.4 %collective-permute-done.5 = f32[1,4,2,3,128]{4,2,1,0,3:T(2,128)S(1)} collective-permute-done((f32[1,4,2,3,128]{4,2,1,0,3:T(2,128)S(1)}, f32[1,4,2,3,128]{4,2,1,0,3:T(2,128)S(1)}, u32[]{:S(2)}, u32[]{:S(2)}) %collective-permute-start.5) | collective-permute-done | bytes 12320 | tf_op jit(solution)/shard_map/ppermute | solution.py:33
  158.1 0.0 copy-start.1
  158.1 0.6 copy-done.1
  (16 shorter events, 0.2 us)
Async XLA Ops:
  0.6 0.9 copy-start.3
  0.6 0.9 copy-start
  1.7 7.0 %collective-permute-start = (f32[1,4,2,8,128]{4,3,2,1,0:T(8,128)S(1)}, f32[1,4,2,8,128]{4,3,2,1,0:T(8,128)S(1)}, u32[]{:S(2)}, u32[]{:S(2)}) collective-permute-start(f32[1,4,2,8,128]{4,3,2,1,0:T(8,128)S(1)} %slice.159), channel_id=1, source_target_pairs={{0,672},{96,0},{192,96},{288,192},{384,288},{480,384},{576,480},{6... | collective-permute-start | bytes 98312 | tf_op jit(solution)/shard_map/ppermute | solution.py:33
  8.7 8.0 %collective-permute-start.1 = (f32[3,1,2,8,128]{4,3,2,1,0:T(8,128)S(1)}, f32[3,1,2,8,128]{4,3,2,1,0:T(8,128)S(1)}, u32[]{:S(2)}, u32[]{:S(2)}) collective-permute-start(f32[3,1,2,8,128]{4,3,2,1,0:T(8,128)S(1)} %pad_maximum_fusion.3), channel_id=1, source_target_pairs={{0,84},{12,0},{24,12},{36,24},{48,36},{60,48},{72,60},{84,72},{1,8... | collective-permute-start | bytes 73736 | tf_op jit(solution)/shard_map/ppermute | solution.py:33
  16.7 7.6 %collective-permute-start.2 = (f32[3,5,1,8,128]{4,3,2,1,0:T(8,128)S(1)}, f32[3,5,1,8,128]{4,3,2,1,0:T(8,128)S(1)}, u32[]{:S(2)}, u32[]{:S(2)}) collective-permute-start(f32[3,5,1,8,128]{4,3,2,1,0:T(8,128)S(1)} %pad_maximum_fusion.1), channel_id=1, source_target_pairs={{0,11},{1,0},{2,1},{3,2},{4,3},{5,4},{6,5},{7,6},{8,7},{9,8},{10,9... | collective-permute-start | bytes 184328 | tf_op jit(solution)/shard_map/ppermute | solution.py:33
  22.4 0.7 copy-start.4
  22.4 0.7 copy-start.5
  22.4 0.7 copy-start.6
  79.7 15.8 %collective-permute-start.3 = (f32[3,5,1,3,128]{4,2,1,0,3:T(1,128)S(1)}, f32[3,5,1,3,128]{4,2,1,0,3:T(1,128)S(1)}, u32[]{:S(2)}, u32[]{:S(2)}) collective-permute-start(f32[3,5,1,3,128]{4,2,1,0,3:T(1,128)S(1)} %copy.18), channel_id=1, source_target_pairs={{0,1},{1,2},{2,3},{3,4},{4,5},{5,6},{6,7},{7,8},{8,9},{9,10},{10,1... | collective-permute-start | bytes 69128 | tf_op jit(solution)/shard_map/ppermute | solution.py:33
  95.6 2.0 %copy-start.2 = (f32[2,8,128]{2,1,0:T(8,128)S(1)}, f32[2,8,128]{2,1,0:T(8,128)}, u32[]{:S(2)}) copy-start(f32[2,8,128]{2,1,0:T(8,128)} %get-tuple-element.41) | copy-start | bytes 24580
  95.7 55.6 %collective-permute-start.4 = (f32[3,1,2,3,128]{4,2,1,0,3:T(2,128)S(1)}, f32[3,1,2,3,128]{4,2,1,0,3:T(2,128)S(1)}, u32[]{:S(2)}, u32[]{:S(2)}) collective-permute-start(f32[3,1,2,3,128]{4,2,1,0,3:T(2,128)S(1)} %slice.165), channel_id=1, source_target_pairs={{0,12},{12,24},{24,36},{36,48},{48,60},{60,72},{72,84},{84,0},{1,1... | collective-permute-start | bytes 27656 | tf_op jit(solution)/shard_map/ppermute | solution.py:33
  151.3 6.8 %collective-permute-start.5 = (f32[1,4,2,3,128]{4,2,1,0,3:T(2,128)S(1)}, f32[1,4,2,3,128]{4,2,1,0,3:T(2,128)S(1)}, u32[]{:S(2)}, u32[]{:S(2)}) collective-permute-start(f32[1,4,2,3,128]{4,2,1,0,3:T(2,128)S(1)} %slice.168), channel_id=1, source_target_pairs={{0,96},{96,192},{192,288},{288,384},{384,480},{480,576},{576,672},... | collective-permute-start | bytes 36872 | tf_op jit(solution)/shard_map/ppermute | solution.py:33
  158.1 0.6 copy-start.1

commit v2 on v1

--- a/solution.py
+++ b/solution.py
@@ -10,11 +10,13 @@
 
 GY = ("gy_0", "gy_1")
 GZ = ("gz_0", "gz_1")
-GX_GY_GZ = ("gx", "gy_0", "gy_1", "gz_0", "gz_1")
+GX_GY = ("gx", "gy_0", "gy_1")
 
 soft_core = 0.09
 cut_sq = 1.0 + soft_core
 far_away = 2.0
+AHEAD = 2
+BEHIND = 1
 corner_pairs = [
     (first_corner, second_corner)
     for first_corner in range(8)
@@ -31,10 +33,6 @@
     count = lax.axis_size(axis)
     pairs = [(source, (source + steps) % count) for source in range(count)]
     return lax.ppermute(value, axis, pairs)
-
-
-def one_axis_at_a_time(value, axes):
-    return functools.reduce(lax.psum, axes, value)
 
 
 def fill_tables(param_ref, table_ref):
@@ -124,7 +122,7 @@
     kind_ref[cell] = jnp.transpose(jnp.broadcast_to(atoms[3:4], (128, 128)))
 
 
-def pair_kernel(sizes, param_ref, cell_ref, force_ref, total_ref, column_ref, row_ref, kind_ref, table_ref, sum_ref):
+def pair_kernel(sizes, param_ref, cell_ref, force_ref, total_ref, column_ref, row_ref, kind_ref, table_ref, sum_ref, square_ref, high_ref, low_ref):
     size_x, size_y, size_z = sizes
     wide_y, wide_z = size_y + 1, size_z + 1
     cells = (size_x + 1) * wide_y * wide_z
@@ -139,10 +137,14 @@
     sum_ref[...] = jnp.zeros_like(sum_ref)
     tile = (8, 128)
 
-    def block(first, second, selfpair, energy):
-        square = lax.dot_general(
-            column_ref[first], row_ref[second], (((1,), (0,)), ((), ())), preferred_element_type=jnp.float32
-        )
+    across = (((1,), (1,)), ((), ()))
+    along = (((1,), (0,)), ((), ()))
+    dot = functools.partial(lax.dot_general, preferred_element_type=jnp.float32)
+
+    def apart(at_pair, first, second):
+        square_ref[at_pair] = dot(column_ref[first], row_ref[second], along)
+
+    def slopes_of(at_pair, first, second, selfpair):
         kind_second = jnp.broadcast_to(cell_ref[second, 3:4], tile) > 0.5
         rows = [
             [
@@ -151,7 +153,6 @@
             ]
             for kind in range(2)
         ]
-        highs, lows = [], []
         partial = jnp.zeros(tile, jnp.float32)
         for pack in range(8):
             slopes = []
@@ -161,7 +162,7 @@
                 attract, repel, coulomb, steep_cut, level = (
                     jnp.where(kind_first, one, zero) for zero, one in zip(*rows)
                 )
-                here = square[at : at + 8]
+                here = square_ref[at_pair, at : at + 8]
                 if selfpair:
                     lane = lax.broadcasted_iota(jnp.int32, tile, 1)
                     sublane = lax.broadcasted_iota(jnp.int32, tile, 0)
@@ -174,20 +175,20 @@
                 slopes.append((steep - steep_cut) * inverse)
             slope = jnp.concatenate(slopes, 0)
             high = slope.astype(jnp.bfloat16)
-            highs.append(high)
-            lows.append((slope - high.astype(jnp.float32)).astype(jnp.bfloat16))
-        high = jnp.concatenate(highs, 0)
-        low = jnp.concatenate(lows, 0)
-        across = (((1,), (1,)), ((), ()))
-        along = (((1,), (0,)), ((), ()))
-        dot = functools.partial(lax.dot_general, preferred_element_type=jnp.float32)
+            high_ref[at_pair, pack * 16 : pack * 16 + 16] = high
+            low_ref[at_pair, pack * 16 : pack * 16 + 16] = (slope - high.astype(jnp.float32)).astype(jnp.bfloat16)
+        return 0.5 * partial if selfpair else partial
+
+    def push(at_pair, first, second, selfpair):
+        high, low = high_ref[at_pair], low_ref[at_pair]
         of_second = row_ref[second, 0:16, :]
         on_first = dot(of_second, high, across) + dot(of_second, low, across)
+        sum_ref[first] = sum_ref[first] + on_first
         if selfpair:
-            return on_first, None, energy + 0.5 * partial
+            return
         of_first = row_ref[first, 0:16, :]
         on_second = dot(of_first, high, along) + dot(of_first, low, along)
-        return on_first, on_second, energy + partial
+        sum_ref[second] = sum_ref[second] + on_second
 
     def one_cell(member, energy):
         base = (
@@ -195,19 +196,23 @@
             + member // size_z % size_y * wide_z
             + member % size_z
         )
+        pairs = []
         for first_corner, second_corner in corner_pairs:
             first, second = (
                 base + x * (wide_y * wide_z) + y * wide_z + z
                 for x, y, z in (corner_of(first_corner), corner_of(second_corner))
             )
-            on_first, on_second, energy = block(first, second, first_corner == second_corner, energy)
-            sum_ref[first] = sum_ref[first] + on_first
-            if on_second is not None:
-                sum_ref[second] = sum_ref[second] + on_second
+            pairs.append((len(pairs), first, second, first_corner == second_corner))
+        for step in range(len(pairs) + AHEAD + BEHIND):
+            if step < len(pairs):
+                apart(*pairs[step][:3])
+            if 0 <= step - AHEAD < len(pairs):
+                energy = energy + slopes_of(*pairs[step - AHEAD])
+            if step >= AHEAD + BEHIND:
+                push(*pairs[step - AHEAD - BEHIND])
         return energy
 
     energy = lax.fori_loop(0, size_x * size_y * size_z, one_cell, jnp.zeros(tile, jnp.float32))
-    total_ref[0] = energy
     virial = jnp.zeros((1, 128), jnp.float32)
     row = lax.broadcasted_iota(jnp.int32, tile, 0)
     for cell in range(cells):
@@ -225,16 +230,17 @@
         crossed = lower[4:5] + lower[5:6] + lower[6:7]
         virial = virial + (norm * slopes + crossed - 2.0 * jnp.sum(spot * moved, 0, keepdims=True))
         force_ref[cell] = spot * slopes - moved
-    total_ref[1] = jnp.where(row == 0, jnp.broadcast_to(-0.5 * virial, tile), 0.0)
-
-
-def pair_sums(params, atoms, sizes):
+    lane = lax.broadcasted_iota(jnp.int32, total_ref.shape, 1)
+    total_ref[...] = jnp.where(lane == 0, jnp.sum(energy), jnp.where(lane == 1, -0.5 * jnp.sum(virial), 0.0))
+
+
+def pair_sums(params, atoms, sizes, copies):
     cells = atoms.shape[0]
     return pl.pallas_call(
         functools.partial(pair_kernel, sizes),
         out_shape=(
             jax.ShapeDtypeStruct((cells, 8, 128), jnp.float32),
-            jax.ShapeDtypeStruct((2, 8, 128), jnp.float32),
+            jax.ShapeDtypeStruct((copies, 128), jnp.float32),
         ),
         in_specs=[
             pl.BlockSpec(memory_space=pltpu.SMEM),
@@ -250,6 +256,9 @@
             pltpu.VMEM((cells, 128, 128), jnp.float32),
             pltpu.VMEM((20, 8, 128), jnp.float32),
             pltpu.VMEM((cells, 16, 128), jnp.float32),
+            pltpu.VMEM((len(corner_pairs), 128, 128), jnp.float32),
+            pltpu.VMEM((len(corner_pairs), 128, 128), jnp.bfloat16),
+            pltpu.VMEM((len(corner_pairs), 128, 128), jnp.bfloat16),
         ],
         name="pair_sums",
     )(params, atoms)
@@ -269,7 +278,10 @@
     wide = extended.shape[:3]
     params = jnp.stack([type_charge, type_sigma, type_epsilon])
     forces, sums = pair_sums(
-        params, extended.reshape((-1, 8, width_atoms)), (size_x, size_y, size_z)
+        params,
+        extended.reshape((-1, 8, width_atoms)),
+        (size_x, size_y, size_z),
+        lax.axis_size(GX_GY),
     )
     reaction = forces.reshape(wide + (8, width_atoms))[..., :3, :]
     returned = passed_along(reaction[:, :, size_z:], GZ, 1)
@@ -278,7 +290,9 @@
     reaction = reaction[:, :size_y].at[:, :1].add(returned)
     returned = passed_along(reaction[size_x:], "gx", 1)
     forces = reaction[:size_x].at[:1].add(returned)
-    summed = one_axis_at_a_time(jnp.sum(sums, (1, 2)), GX_GY_GZ)
+    rows = jnp.sum(lax.all_to_all(sums, GX_GY, 0, 0, tiled=True), 0)
+    copies = jnp.broadcast_to(rows, (lax.axis_size(GZ), width_atoms))
+    summed = jnp.sum(lax.all_to_all(copies, GZ, 0, 0, tiled=True), 0)[:2]
     normaliser = 1.0 / (
         size_x
         * lax.axis_size("gx")

time: 159 us -> 115 us (0.72)
  the two profiles are of different devices: /device:TPU:2 before, /device:TPU:1 now
where the time goes in v2:
time: 115 us; the launch traced here: 114 us
  starting transfers between devices  49 us (43%)
  waiting for transfers between devices  29.7 us (26%)
  Pallas kernels  28.4 us (25%)
  local copies, waits for them, and re-layouts  4.17 us (4%)
  other arithmetic  2.06 us (2%)
    ppermute x6, starting transfers between devices, passed_along(): return lax.ppermute(value, axis, pairs)  34.6 us
    pallas_call x1, Pallas kernels, pair_sums(): pl.pallas_call(functools.partial(pair_kernel, sizes), out_shape=(jax.Shap...  28.4 us
    ppermute x6, waiting for transfers between devices, passed_along(): return lax.ppermute(value, axis, pairs)  14.6 us
    all_to_all x1, starting transfers between devices, per_device(): rows = jnp.sum(lax.all_to_all(sums, GX_GY, 0, 0, tiled=True), 0)  11 us
    all_to_all x1, waiting for transfers between devices, per_device(): summed = jnp.sum(lax.all_to_all(copies, GZ, 0, 0, tiled=True), 0)[:2]  8.79 us
    all_to_all x1, waiting for transfers between devices, per_device(): rows = jnp.sum(lax.all_to_all(sums, GX_GY, 0, 0, tiled=True), 0)  6.29 us
    all_to_all x1, starting transfers between devices, per_device(): summed = jnp.sum(lax.all_to_all(copies, GZ, 0, 0, tiled=True), 0)[:2]  3.42 us
  transfers between devices with their start and end apart: 8, of which 6 were waited for; matrix products, arithmetic and copies ran while one was open for 2% of the time, Pallas kernels for 0%

profile of v2, /device:TPU:1, one launch (start us, length us, event | category | flops | bytes accessed | tf_op | source)
XLA Modules:
  0.0 114.2 jit_solution(11558218611584374864)
XLA Ops:
  0.6 0.0 copy-start.2
  0.6 0.0 copy-start
  0.6 0.8 copy.25
  1.4 0.1 compare_convert_fusion
  1.5 0.0 copy-done.2
  1.5 0.0 copy-done
  1.6 0.1 stack.28
  1.7 5.9 %collective-permute-start = (f32[1,4,2,8,128]{4,3,2,1,0:T(8,128)S(1)}, f32[1,4,2,8,128]{4,3,2,1,0:T(8,128)S(1)}, u32[]{:S(2)}, u32[]{:S(2)}) collective-permute-start(f32[1,4,2,8,128]{4,3,2,1,0:T(8,128)S(1)} %slice.163), channel_id=1, source_target_pairs={{0,672},{96,0},{192,96},{288,192},{384,288},{480,384},{576,480},{6... | collective-permute-start | bytes 98312 | tf_op jit(solution)/shard_map/ppermute | solution.py:35
  7.6 1.0 collective-permute-done
  8.6 11.3 %collective-permute-start.1 = (f32[3,1,2,8,128]{4,3,2,1,0:T(8,128)S(1)}, f32[3,1,2,8,128]{4,3,2,1,0:T(8,128)S(1)}, u32[]{:S(2)}, u32[]{:S(2)}) collective-permute-start(f32[3,1,2,8,128]{4,3,2,1,0:T(8,128)S(1)} %pad_maximum_fusion.3), channel_id=1, source_target_pairs={{0,84},{12,0},{24,12},{36,24},{48,36},{60,48},{72,60},{84,72},{1,8... | collective-permute-start | bytes 73736 | tf_op jit(solution)/shard_map/ppermute | solution.py:35
  19.9 0.8 collective-permute-done.1
  20.7 10.4 %collective-permute-start.2 = (f32[3,5,1,8,128]{4,3,2,1,0:T(8,128)S(1)}, f32[3,5,1,8,128]{4,3,2,1,0:T(8,128)S(1)}, u32[]{:S(2)}, u32[]{:S(2)}) collective-permute-start(f32[3,5,1,8,128]{4,3,2,1,0:T(8,128)S(1)} %pad_maximum_fusion.1), channel_id=1, source_target_pairs={{0,11},{1,0},{2,1},{3,2},{4,3},{5,4},{6,5},{7,6},{8,7},{9,8},{10,9... | collective-permute-start | bytes 184328 | tf_op jit(solution)/shard_map/ppermute | solution.py:35
  31.1 0.0 copy-start.3
  31.1 0.0 copy-start.4
  31.1 0.0 copy-start.5
  31.2 0.6 copy-done.3
  31.8 0.0 copy-done.4
  31.8 0.0 copy-done.5
  31.8 0.6 pad_maximum_fusion.4.param_ref
  32.4 3.9 %collective-permute-done.2 = f32[3,5,1,8,128]{4,3,2,1,0:T(8,128)S(1)} collective-permute-done((f32[3,5,1,8,128]{4,3,2,1,0:T(8,128)S(1)}, f32[3,5,1,8,128]{4,3,2,1,0:T(8,128)S(1)}, u32[]{:S(2)}, u32[]{:S(2)}) %collective-permute-start.2) | collective-permute-done | bytes 61472 | tf_op jit(solution)/shard_map/ppermute | solution.py:35
  36.3 0.7 pad_maximum_fusion
  37.0 28.4 %pair_sums.1 = (f32[45,8,128]{2,1,0:T(8,128)}, f32[64,128]{1,0:T(8,128)}) custom-call(f32[3,2]{1,0:T(4,128)} %pad_maximum_fusion.4.param_ref, f32[45,8,128]{2,1,0:T(8,128)} %bitcast.21), custom_call_target="tpu_custom_call" | custom-call | tf_op jit(solution)/shard_map/pair_sums/pallas_call | solution.py:239
  65.4 0.9 fusion.2
  66.3 1.9 %collective-permute-start.3 = (f32[3,5,1,3,128]{4,2,1,0,3:T(1,128)S(1)}, f32[3,5,1,3,128]{4,2,1,0,3:T(1,128)S(1)}, u32[]{:S(2)}, u32[]{:S(2)}) collective-permute-start(f32[3,5,1,3,128]{4,2,1,0,3:T(1,128)S(1)} %copy.36), channel_id=1, source_target_pairs={{0,1},{1,2},{2,3},{3,4},{4,5},{5,6},{6,7},{7,8},{8,9},{9,10},{10,1... | collective-permute-start | bytes 69128 | tf_op jit(solution)/shard_map/ppermute | solution.py:35
  68.3 0.9 slice.164
  69.2 8.8 %collective-permute-done.3 = f32[3,5,1,3,128]{4,2,1,0,3:T(1,128)S(1)} collective-permute-done((f32[3,5,1,3,128]{4,2,1,0,3:T(1,128)S(1)}, f32[3,5,1,3,128]{4,2,1,0,3:T(1,128)S(1)}, u32[]{:S(2)}, u32[]{:S(2)}) %collective-permute-start.3) | collective-permute-done | bytes 23072 | tf_op jit(solution)/shard_map/ppermute | solution.py:35
  78.1 0.1 scatter-add.10
  78.2 1.9 %collective-permute-start.4 = (f32[3,1,2,3,128]{4,2,1,0,3:T(2,128)S(1)}, f32[3,1,2,3,128]{4,2,1,0,3:T(2,128)S(1)}, u32[]{:S(2)}, u32[]{:S(2)}) collective-permute-start(f32[3,1,2,3,128]{4,2,1,0,3:T(2,128)S(1)} %slice.169), channel_id=1, source_target_pairs={{0,12},{12,24},{24,36},{36,48},{48,60},{60,72},{72,84},{84,0},{1,1... | collective-permute-start | bytes 27656 | tf_op jit(solution)/shard_map/ppermute | solution.py:35
  80.1 11.0 %all-to-all-start = ((f32[64,1,128]{2,1,0:T(1,128)}), f32[64,1,128]{2,1,0:T(1,128)S(1)}, u32[]{:S(2)}, u32[]{:S(2)}) async-start(f32[64,1,128]{2,1,0:T(1,128)} %bitcast.15), calls=%async_computation | async-start | bytes 65536 | tf_op jit(solution)/shard_map/all_to_all | solution.py:293
  91.1 0.0 collective-permute-done.4
  91.2 3.3 %collective-permute-start.5 = (f32[1,4,2,3,128]{4,2,1,0,3:T(2,128)S(1)}, f32[1,4,2,3,128]{4,2,1,0,3:T(2,128)S(1)}, u32[]{:S(2)}, u32[]{:S(2)}) collective-permute-start(f32[1,4,2,3,128]{4,2,1,0,3:T(2,128)S(1)} %slice.172), channel_id=1, source_target_pairs={{0,96},{96,192},{192,288},{288,384},{384,480},{480,576},{576,672},... | collective-permute-start | bytes 36872 | tf_op jit(solution)/shard_map/ppermute | solution.py:35
  94.4 6.3 %all-to-all-done = f32[64,1,128]{2,1,0:T(1,128)S(1)} async-done(((f32[64,1,128]{2,1,0:T(1,128)}), f32[64,1,128]{2,1,0:T(1,128)S(1)}, u32[]{:S(2)}, u32[]{:S(2)}) %all-to-all-start) | async-done | bytes 32800 | tf_op jit(solution)/shard_map/all_to_all | solution.py:293
  100.7 0.1 reduce_sum.18
  100.8 0.6 broadcast_in_dim.4
  101.4 3.4 %all-to-all-start.1 = ((f32[12,1,128]{2,1,0:T(1,128)}), f32[12,1,128]{2,1,0:T(1,128)S(1)}, u32[]{:S(2)}, u32[]{:S(2)}) async-start(f32[12,1,128]{2,1,0:T(1,128)} %broadcast_in_dim.4), calls=%async_computation.1 | async-start | bytes 12288 | tf_op jit(solution)/shard_map/all_to_all | solution.py:295
  104.8 0.0 collective-permute-done.5
  104.9 0.0 copy-start.1
  104.9 8.8 %all-to-all-done.1 = f32[12,1,128]{2,1,0:T(1,128)S(1)} async-done(((f32[12,1,128]{2,1,0:T(1,128)}), f32[12,1,128]{2,1,0:T(1,128)S(1)}, u32[]{:S(2)}, u32[]{:S(2)}) %all-to-all-start.1) | async-done | bytes 6176 | tf_op jit(solution)/shard_map/all_to_all | solution.py:295
  113.7 0.5 slice_multiply_fusion
  114.2 0.0 copy-done.1
  (17 shorter events, 0.2 us)
Async XLA Ops:
  0.6 0.9 copy-start.2
  0.6 0.9 copy-start
  1.7 6.9 %collective-permute-start = (f32[1,4,2,8,128]{4,3,2,1,0:T(8,128)S(1)}, f32[1,4,2,8,128]{4,3,2,1,0:T(8,128)S(1)}, u32[]{:S(2)}, u32[]{:S(2)}) collective-permute-start(f32[1,4,2,8,128]{4,3,2,1,0:T(8,128)S(1)} %slice.163), channel_id=1, source_target_pairs={{0,672},{96,0},{192,96},{288,192},{384,288},{480,384},{576,480},{6... | collective-permute-start | bytes 98312 | tf_op jit(solution)/shard_map/ppermute | solution.py:35
  8.6 12.1 %collective-permute-start.1 = (f32[3,1,2,8,128]{4,3,2,1,0:T(8,128)S(1)}, f32[3,1,2,8,128]{4,3,2,1,0:T(8,128)S(1)}, u32[]{:S(2)}, u32[]{:S(2)}) collective-permute-start(f32[3,1,2,8,128]{4,3,2,1,0:T(8,128)S(1)} %pad_maximum_fusion.3), channel_id=1, source_target_pairs={{0,84},{12,0},{24,12},{36,24},{48,36},{60,48},{72,60},{84,72},{1,8... | collective-permute-start | bytes 73736 | tf_op jit(solution)/shard_map/ppermute | solution.py:35
  20.7 15.6 %collective-permute-start.2 = (f32[3,5,1,8,128]{4,3,2,1,0:T(8,128)S(1)}, f32[3,5,1,8,128]{4,3,2,1,0:T(8,128)S(1)}, u32[]{:S(2)}, u32[]{:S(2)}) collective-permute-start(f32[3,5,1,8,128]{4,3,2,1,0:T(8,128)S(1)} %pad_maximum_fusion.1), channel_id=1, source_target_pairs={{0,11},{1,0},{2,1},{3,2},{4,3},{5,4},{6,5},{7,6},{8,7},{9,8},{10,9... | collective-permute-start | bytes 184328 | tf_op jit(solution)/shard_map/ppermute | solution.py:35
  31.1 0.7 copy-start.3
  31.1 0.7 copy-start.4
  31.1 0.7 copy-start.5
  66.3 11.7 %collective-permute-start.3 = (f32[3,5,1,3,128]{4,2,1,0,3:T(1,128)S(1)}, f32[3,5,1,3,128]{4,2,1,0,3:T(1,128)S(1)}, u32[]{:S(2)}, u32[]{:S(2)}) collective-permute-start(f32[3,5,1,3,128]{4,2,1,0,3:T(1,128)S(1)} %copy.36), channel_id=1, source_target_pairs={{0,1},{1,2},{2,3},{3,4},{4,5},{5,6},{6,7},{7,8},{8,9},{9,10},{10,1... | collective-permute-start | bytes 69128 | tf_op jit(solution)/shard_map/ppermute | solution.py:35
  78.2 12.9 %collective-permute-start.4 = (f32[3,1,2,3,128]{4,2,1,0,3:T(2,128)S(1)}, f32[3,1,2,3,128]{4,2,1,0,3:T(2,128)S(1)}, u32[]{:S(2)}, u32[]{:S(2)}) collective-permute-start(f32[3,1,2,3,128]{4,2,1,0,3:T(2,128)S(1)} %slice.169), channel_id=1, source_target_pairs={{0,12},{12,24},{24,36},{36,48},{48,60},{60,72},{72,84},{84,0},{1,1... | collective-permute-start | bytes 27656 | tf_op jit(solution)/shard_map/ppermute | solution.py:35
  80.1 20.6 %all-to-all-start = ((f32[64,1,128]{2,1,0:T(1,128)}), f32[64,1,128]{2,1,0:T(1,128)S(1)}, u32[]{:S(2)}, u32[]{:S(2)}) async-start(f32[64,1,128]{2,1,0:T(1,128)} %bitcast.15), calls=%async_computation | async-start | bytes 65536 | tf_op jit(solution)/shard_map/all_to_all | solution.py:293
  91.2 13.7 %collective-permute-start.5 = (f32[1,4,2,3,128]{4,2,1,0,3:T(2,128)S(1)}, f32[1,4,2,3,128]{4,2,1,0,3:T(2,128)S(1)}, u32[]{:S(2)}, u32[]{:S(2)}) collective-permute-start(f32[1,4,2,3,128]{4,2,1,0,3:T(2,128)S(1)} %slice.172), channel_id=1, source_target_pairs={{0,96},{96,192},{192,288},{288,384},{384,480},{480,576},{576,672},... | collective-permute-start | bytes 36872 | tf_op jit(solution)/shard_map/ppermute | solution.py:35
  101.4 12.3 %all-to-all-start.1 = ((f32[12,1,128]{2,1,0:T(1,128)}), f32[12,1,128]{2,1,0:T(1,128)S(1)}, u32[]{:S(2)}, u32[]{:S(2)}) async-start(f32[12,1,128]{2,1,0:T(1,128)} %broadcast_in_dim.4), calls=%async_computation.1 | async-start | bytes 12288 | tf_op jit(solution)/shard_map/all_to_all | solution.py:295
  104.9 9.4 %copy-start.1 = (f32[2,4,2,3,128]{4,2,1,0,3:T(2,128)}, f32[2,4,2,3,128]{4,2,1,0,3:T(2,128)S(1)}, u32[]{:S(2)}) copy-start(f32[2,4,2,3,128]{4,2,1,0,3:T(2,128)S(1)} %fusion) | copy-start | bytes 73732

commit v3 on v2

v3 whole, which is shorter than its diff:
```python
import dataclasses
import functools
import itertools

import jax
import jax.numpy as jnp
from jax import lax
from jax.experimental import pallas as pl
from jax.experimental.pallas import tpu as pltpu
from jax.sharding import Mesh
from jax.sharding import PartitionSpec as P

GY = ("gy_0", "gy_1")
GZ = ("gz_0", "gz_1")
ONE = ("gx", "gz_1")
OTHER = ("gy_0", "gy_1", "gz_0")

soft_core = 0.09
cut_sq = 1.0 + soft_core
far_away = 2.0
GROUP = 12
corner_pairs = [
    (first_corner, second_corner)
    for first_corner in range(8)
    for second_corner in range(8)
    if first_corner & second_corner == 0 and first_corner <= second_corner
]


def corner_of(which):
    return (which & 1, which >> 1 & 1, which >> 2 & 1)


def passed_along(value, axis, steps):
    count = lax.axis_size(axis)
    pairs = [(source, (source + steps) % count) for source in range(count)]
    return lax.ppermute(value, axis, pairs)


def fill_tables(param_ref, coef_ref):
    tile = (8, 128)
    charge = [jnp.full(tile, param_ref[0, kind], jnp.float32) for kind in range(2)]
    sigma = [jnp.full(tile, param_ref[1, kind], jnp.float32) for kind in range(2)]
    root = [jnp.sqrt(jnp.full(tile, param_ref[2, kind], jnp.float32)) for kind in range(2)]
    for first in range(2):
        for second in range(2):
            width = 0.5 * (sigma[first] + sigma[second])
            width_six = (width * width) * (width * width) * (width * width)
            attract = 24.0 * (root[first] * root[second]) * width_six
            repel = attract * width_six
            coulomb = charge[first] * charge[second]
            value, steep, _ = pair_parts(jnp.full(tile, cut_sq, jnp.float32), attract, repel, coulomb)
            level = -value
            for at, entry in enumerate((attract, repel, coulomb, steep, level)):
                coef_ref[(first * 2 + second) * 5 + at] = entry


def pair_parts(square, attract, repel, coulomb):
    inverse = lax.rsqrt(square)
    two = inverse * inverse
    six = (two * two) * two
    pulled = attract * six
    pushed = repel * (six * six)
    lennard = pushed - pulled
    charged = coulomb * inverse
    moment = (lennard + pushed) + charged
    return (lennard * (1.0 / 6.0) + charged) + moment, moment * inverse, inverse


def fill_cell(cell_ref, column_ref, row_ref, kind_ref, cell, place, as_first):
    atoms = cell_ref[cell]
    row = lax.broadcasted_iota(jnp.int32, (8, 128), 0)
    shift = jnp.where(row == 0, place[0], jnp.where(row == 1, place[1], place[2]))
    spot = jnp.where(row < 3, atoms + shift, 0.0)
    norm = jnp.sum(spot * spot, 0, keepdims=True) + 0.5 * soft_core + far_away * (1.0 - atoms[4:5])
    whole = jnp.where(row == 3, jnp.broadcast_to(norm, (8, 128)), spot)
    high = whole.astype(jnp.bfloat16).astype(jnp.float32)
    middle = (whole - high).astype(jnp.bfloat16).astype(jnp.float32)
    low = ((whole - high) - middle).astype(jnp.bfloat16).astype(jnp.float32)

    def down(value, by):
        return pltpu.roll(value, by, 0)

    xyz = row < 3
    xyz_down = (row > 3) & (row < 7)
    middle_down = jnp.where(xyz_down, down(middle, 4), 0.0)
    rows = [
        jnp.where(xyz, high, jnp.where(xyz_down, middle_down, 1.0)),
        jnp.where(
            xyz,
            low,
            jnp.where(
                row == 3,
                1.0,
                jnp.where(
                    row == 4,
                    down(high, 1),
                    jnp.where(row == 5, down(middle, 2), jnp.where(row == 6, down(low, 3), 0.0)),
                ),
            ),
        ),
        jnp.where(xyz, high, middle_down),
        jnp.where(xyz, high, 0.0),
    ]
    row_ref[cell] = jnp.concatenate(rows, 0).astype(jnp.bfloat16)
    if not as_first:
        return
    high_two = -2.0 * high
    middle_two = -2.0 * middle
    columns = [
        jnp.where(
            row < 4,
            jnp.where(xyz, high_two, high),
            down(jnp.where(xyz, high_two, middle), 4),
        ),
        jnp.where(xyz, high_two, jnp.where(row == 3, low, jnp.where(row == 7, 0.0, 1.0))),
        jnp.where(xyz, middle_two, jnp.where(xyz_down, down(middle_two, 4), 0.0)),
        jnp.where(xyz, -2.0 * low, 0.0),
    ]
    columns[3] = jnp.where(row == 7, jnp.broadcast_to(atoms[3:4], (8, 128)), columns[3])
    turned = jnp.transpose(jnp.concatenate(columns, 0))
    column_ref[cell] = turned.astype(jnp.bfloat16)
    kind_ref[cell] = jnp.broadcast_to(turned[:, 31:32], (128, 128))


def pair_kernel(plan, *refs):
    refs = list(refs)
    param_ref, table_ref, cell_ref = refs[:3]
    refs = refs[3:]
    before_ref = refs.pop(0) if plan.added else None
    force_ref, total_ref, sum_ref, column_ref, row_ref, kind_ref, coef_ref, square_ref, high_ref, low_ref = refs
    cells = len(plan.places)
    tile = (8, 128)
    fill_tables(param_ref, coef_ref)
    for cell in range(cells):
        fill_cell(cell_ref, column_ref, row_ref, kind_ref, cell, plan.places[cell], plan.firsts[cell])
    sum_ref[...] = jnp.zeros_like(sum_ref)
    energy = jnp.zeros(tile, jnp.float32)

    across = (((1,), (1,)), ((), ()))
    along = (((1,), (0,)), ((), ()))
    dot = functools.partial(lax.dot_general, preferred_element_type=jnp.float32)

    def apart(slot, first, second):
        square_ref[slot] = dot(column_ref[first], row_ref[second], along)

    def slopes_of(slot, first, second, selfpair):
        kind_second = jnp.broadcast_to(cell_ref[second, 3:4], tile) > 0.5
        rows = [
            [
                jnp.where(kind_second, coef_ref[(kind * 2 + 1) * 5 + at], coef_ref[kind * 2 * 5 + at])
                for at in range(5)
            ]
            for kind in range(2)
        ]
        partial = jnp.zeros(tile, jnp.float32)
        for pack in range(8):
            slopes = []
            for half in range(2):
                at = pack * 16 + half * 8
                kind_first = kind_ref[first, at : at + 8, :] > 0.5
                attract, repel, coulomb, steep_cut, level = (
                    jnp.where(kind_first, one, zero) for zero, one in zip(*rows)
                )
                here = square_ref[slot, at : at + 8]
                if selfpair:
                    lane = lax.broadcasted_iota(jnp.int32, tile, 1)
                    sublane = lax.broadcasted_iota(jnp.int32, tile, 0)
                    here = jnp.where(lane == sublane + at, cut_sq, here)
                value, steep, inverse = pair_parts(jnp.minimum(here, cut_sq), attract, repel, coulomb)
                partial = partial + (value + level)
                slopes.append((steep - steep_cut) * inverse)
            slope = jnp.concatenate(slopes, 0)
            high = slope.astype(jnp.bfloat16)
            high_ref[slot, pack * 16 : pack * 16 + 16] = high
            low_ref[slot, pack * 16 : pack * 16 + 16] = (slope - high.astype(jnp.float32)).astype(jnp.bfloat16)
        return 0.5 * partial if selfpair else partial

    def push(slot, first, second, selfpair):
        high, low = high_ref[slot], low_ref[slot]
        of_second = row_ref[second, 0:16, :]
        on_first = dot(of_second, high, across) + dot(of_second, low, across)
        sum_ref[first] = sum_ref[first] + on_first
        if selfpair:
            return
        of_first = row_ref[first, 0:16, :]
        on_second = dot(of_first, high, along) + dot(of_first, low, along)
        sum_ref[second] = sum_ref[second] + on_second

    def run(start, rounds, group, selfpair, energy):
        if not rounds:
            return energy

        def cells_of(at):
            return table_ref[2 * at], table_ref[2 * at + 1]

        for slot in range(group):
            apart(slot, *cells_of(start + slot))
        high_ref[group - 1] = jnp.zeros((128, 128), jnp.bfloat16)
        low_ref[group - 1] = jnp.zeros((128, 128), jnp.bfloat16)

        def one_round(index, energy):
            base = start + index * group
            following = start + jnp.minimum(index + 1, rounds - 1) * group
            for slot in range(group):
                energy = energy + slopes_of(slot, *cells_of(base + slot), selfpair)
                apart(slot, *cells_of(following + slot))
                if slot:
                    push(slot - 1, *cells_of(base + slot - 1), selfpair)
                else:
                    push(group - 1, *cells_of(jnp.maximum(base - 1, start)), selfpair)
            return energy

        energy = lax.fori_loop(0, rounds, one_round, energy)
        push(group - 1, *cells_of(start + rounds * group - 1), selfpair)
        return energy

    start = 0
    for rounds, group, selfpair in plan.runs:
        energy = run(start, rounds, group, selfpair, energy)
        start += rounds * group
    moment = jnp.zeros((1, 128), jnp.float32)
    steepness = jnp.zeros((1, 128), jnp.float32)
    row = lax.broadcasted_iota(jnp.int32, tile, 0)
    for cell in range(cells):
        place = plan.places[cell]
        shift = jnp.where(row == 0, place[0], jnp.where(row == 1, place[1], place[2]))
        spot = jnp.where(row < 3, cell_ref[cell] + shift, 0.0)
        upper, lower = sum_ref[cell, 0:8, :], sum_ref[cell, 8:16, :]
        moved = jnp.where(row < 3, upper + pltpu.roll(upper, 4, 0) + lower, 0.0)
        slopes = upper[3:4]
        norm = (
            jnp.sum(spot * spot, 0, keepdims=True)
            + 0.5 * soft_core
            + far_away * (1.0 - cell_ref[cell, 4:5])
        )
        crossed = lower[4:5] + lower[5:6] + lower[6:7]
        moment = moment + (norm * slopes + crossed - 2.0 * jnp.sum(spot * moved, 0, keepdims=True))
        steepness = steepness + slopes
        force_ref[cell] = spot * slopes - moved
    lane = lax.broadcasted_iota(jnp.int32, total_ref.shape, 1)
    virial = 0.5 * (soft_core * jnp.sum(steepness) - jnp.sum(moment))
    total = jnp.where(
        lane == 0, jnp.sum(energy) - 0.5 * jnp.sum(moment), jnp.where(lane == 1, virial, 0.0)
    )
    total_ref[...] = total + before_ref[0:1] if plan.added else total


@dataclasses.dataclass(frozen=True)
class Plan:
    places: tuple
    firsts: tuple
    runs: tuple
    added: bool
    copies: int


def rounds_of(pairs, group):
    if not pairs:
        return ()
    group = max(g for g in range(1, group + 1) if len(pairs) % g == 0)
    return ((len(pairs) // group, group, pairs[0][0] == pairs[0][1]),)


def pair_sums(plan, table, params, atoms, *before):
    cells = len(plan.places)
    vmem = pl.BlockSpec(memory_space=pltpu.VMEM)
    smem = pl.BlockSpec(memory_space=pltpu.SMEM)
    slots = max(group for _, group, _ in plan.runs)
    sums = (cells, 16, 128)
    shapes = [(cells, 8, 128), (plan.copies, 128)]
    return pl.pallas_call(
        functools.partial(pair_kernel, plan),
        out_shape=tuple(jax.ShapeDtypeStruct(shape, jnp.float32) for shape in shapes),
        in_specs=[smem, smem, vmem] + [vmem] * len(before),
        out_specs=(vmem, vmem),
        scratch_shapes=[
            pltpu.VMEM(sums, jnp.float32),
            pltpu.VMEM((cells, 128, 32), jnp.bfloat16),
            pltpu.VMEM((cells, 32, 128), jnp.bfloat16),
            pltpu.VMEM((cells, 128, 128), jnp.float32),
            pltpu.VMEM((20, 8, 128), jnp.float32),
            pltpu.VMEM((slots, 128, 128), jnp.float32),
            pltpu.VMEM((slots, 128, 128), jnp.bfloat16),
            pltpu.VMEM((slots, 128, 128), jnp.bfloat16),
        ],
        name="pair_sums",
    )(params, jnp.array(table, jnp.int32).reshape(-1), atoms, *before)


def pair_lists(sizes):
    alone, inside, beyond = [], [], []
    for member in itertools.product(*map(range, sizes)):
        for corners in corner_pairs:
            pair = tuple(tuple(m + c for m, c in zip(member, corner_of(which))) for which in corners)
            if pair[0] == pair[1]:
                alone.append(pair)
            elif all(at < size for cell in pair for at, size in zip(cell, sizes)):
                inside.append(pair)
            else:
                beyond.append(pair)
    return alone, inside, beyond


def flat(cell, grid):
    return (cell[0] * grid[1] + cell[1]) * grid[2] + cell[2]


def plans_of(sizes, copies):
    wide = tuple(size + 1 for size in sizes)
    alone, inside, beyond = pair_lists(sizes)

    def places(grid):
        return tuple(
            tuple(float(at) - (size + 1) / 2 for at, size in zip(cell, sizes))
            for cell in itertools.product(*map(range, grid))
        )

    own = list(itertools.product(*map(range, sizes)))
    near = Plan(
        places(sizes),
        (True,) * len(own),
        rounds_of(alone, GROUP) + rounds_of(inside, GROUP),
        False,
        8,
    )
    everywhere = list(itertools.product(*map(range, wide)))
    starters = {pair[0] for pair in beyond}
    far = Plan(
        places(wide),
        tuple(cell in starters for cell in everywhere),
        rounds_of(beyond, GROUP),
        True,
        copies,
    )
    near_table = [tuple(flat(cell, sizes) for cell in pair) for pair in alone + inside]
    far_table = [tuple(flat(cell, wide) for cell in pair) for pair in beyond]
    return (near, near_table), (far, far_table)


def per_device(positions, type_ids, counts, type_charge, type_sigma, type_epsilon):
    size_x, size_y, size_z, width_atoms = positions.shape[1:]
    slots = lax.broadcasted_iota(jnp.int32, type_ids.shape, 3)
    occupied = (slots < counts[..., None]).astype(jnp.float32)
    blank = jnp.zeros(type_ids.shape, jnp.float32)
    atoms = jnp.stack(
        [positions[0], positions[1], positions[2], type_ids.astype(jnp.float32), occupied, blank, blank, blank], 3
    )
    sizes = (size_x, size_y, size_z)
    params = jnp.stack([type_charge, type_sigma, type_epsilon])
    (near, near_table), (far, far_table) = plans_of(sizes, lax.axis_size(ONE))
    own = atoms.reshape((-1, 8, width_atoms))
    extended = jnp.concatenate([atoms, passed_along(atoms[:1], "gx", -1)], 0)
    extended = jnp.concatenate([extended, passed_along(extended[:, :1], GY, -1)], 1)
    own, extended = lax.optimization_barrier((own, extended))
    edge = passed_along(extended[:, :, :1], GZ, -1)
    inner, inner_sums = pair_sums(near, near_table, params, own)
    edge, inner, inner_sums = lax.optimization_barrier((edge, inner, inner_sums))
    extended = jnp.concatenate([extended, edge], 2)
    wide = extended.shape[:3]
    forces, sums = pair_sums(far, far_table, params, extended.reshape((-1, 8, width_atoms)), inner_sums)
    inner = inner.reshape(sizes + (8, width_atoms))[..., :3, :]
    reaction = forces.reshape(wide + (8, width_atoms))[..., :3, :]
    returned = passed_along(reaction[:, :, size_z:], GZ, 1)
    rows = jnp.sum(lax.all_to_all(sums, ONE, 0, 0, tiled=True), 0)
    returned, rows = lax.optimization_barrier((returned, rows))
    reaction = reaction[:, :, :size_z].at[:, :, :1].add(returned)
    returned = passed_along(reaction[:, size_y:], GY, 1)
    copies = jnp.broadcast_to(rows, (lax.axis_size(OTHER), width_atoms))
    summed = jnp.sum(lax.all_to_all(copies, OTHER, 0, 0, tiled=True), 0)[:2]
    reaction = reaction[:, :size_y].at[:, :1].add(returned)
    returned = passed_along(reaction[size_x:], "gx", 1)
    forces = reaction[:size_x].at[:1].add(returned) + inner
    normaliser = 1.0 / (
        size_x
        * lax.axis_size("gx")
        * size_y
        * lax.axis_size(GY)
        * size_z
        * lax.axis_size(GZ)
        * width_atoms
    )
    return (jnp.transpose(forces, (3, 0, 1, 2, 4)), summed * normaliser)


def solution(mesh):
    split = Mesh(
        mesh.devices.reshape(mesh.shape["gx"], 4, 2, 3, 4), ("gx", "gy_0", "gy_1", "gz_0", "gz_1")
    )
    placed = (P(None, "gx", GY, GZ, None), P("gx", GY, GZ, None), P("gx", GY, GZ), P(), P(), P())
    return jax.shard_map(
        per_device,
        mesh=split,
        in_specs=placed,
        out_specs=(P(None, "gx", GY, GZ, None), P()),
        check_vma=False,
    )
```

time: 115 us -> 104 us (0.904)
  waiting for transfers between devices: 29.7 us -> 17.1 us
  starting transfers between devices: 49 us -> 52.4 us
  Pallas kernels: 28.4 us -> 25.6 us
    ppermute x6, waiting for transfers between devices: 14.6 us -> 4.76 us  [passed_along(): return lax.ppermute(value, axis, pairs)]
    ppermute x6, starting transfers between devices: 34.6 us -> 38.1 us  [passed_along(): return lax.ppermute(value, axis, pairs)]
    pallas_call x1 -> x2, Pallas kernels: 28.4 us -> 25.6 us  [pair_sums(): pl.pallas_call(functools.partial(pair_kernel, plan), out_shape=tuple((jax...]
    all_to_all x2, waiting for transfers between devices: 15.1 us -> 12.4 us  [the longest x1 8.82 us: per_device(): summed = jnp.sum(lax.all_to_all(copies, OTHER, 0, 0, tiled=True), 0)[:2]]
  transfers between devices with their start and end apart: 8 -> 8, of which waited for: 6 -> 5; matrix products, arithmetic and copies ran while one was open for 2% -> 4% of each run, Pallas kernels for 0% -> 10%
where the time goes in v3:
time: 104 us
  starting transfers between devices  52.4 us (50%)
  Pallas kernels  25.6 us (25%)
  waiting for transfers between devices  17.1 us (16%)
  local copies, waits for them, and re-layouts  4.98 us (5%)
  other arithmetic  2.72 us (3%)
    ppermute x6, starting transfers between devices, passed_along(): return lax.ppermute(value, axis, pairs)  38.1 us
    pallas_call x2, Pallas kernels, pair_sums(): pl.pallas_call(functools.partial(pair_kernel, plan), out_shape=tuple((jax...  25.6 us
    all_to_all x1, waiting for transfers between devices, per_device(): summed = jnp.sum(lax.all_to_all(copies, OTHER, 0, 0, tiled=True), 0)[:2]  8.82 us
    all_to_all x1, starting transfers between devices, per_device(): summed = jnp.sum(lax.all_to_all(copies, OTHER, 0, 0, tiled=True), 0)[:2]  8.23 us
    all_to_all x1, starting transfers between devices, per_device(): rows = jnp.sum(lax.all_to_all(sums, ONE, 0, 0, tiled=True), 0)  6.06 us
    ppermute x6, waiting for transfers between devices, passed_along(): return lax.ppermute(value, axis, pairs)  4.76 us
    all_to_all x1, waiting for transfers between devices, per_device(): rows = jnp.sum(lax.all_to_all(sums, ONE, 0, 0, tiled=True), 0)  3.54 us
  transfers between devices with their start and end apart: 8, of which 5 were waited for; matrix products, arithmetic and copies ran while one was open for 4% of the time, Pallas kernels for 10%

profile of v3, /device:TPU:1, one launch (start us, length us, event | category | flops | bytes accessed | tf_op | source)
XLA Modules:
  0.0 103.7 jit_solution(15973063294003728168)
XLA Ops:
  0.6 0.0 copy-start.2
  0.6 0.0 copy-start
  0.6 0.8 copy.52
  1.4 0.1 compare_convert_fusion
  1.5 0.0 copy-done.2
  1.5 0.0 copy-done
  1.6 0.1 stack.46
  1.7 5.9 %collective-permute-start = (f32[1,4,2,8,128]{4,3,2,1,0:T(8,128)S(1)}, f32[1,4,2,8,128]{4,3,2,1,0:T(8,128)S(1)}, u32[]{:S(2)}, u32[]{:S(2)}) collective-permute-start(f32[1,4,2,8,128]{4,3,2,1,0:T(8,128)S(1)} %slice.167), channel_id=1, source_target_pairs={{0,672},{96,0},{192,96},{288,192},{384,288},{480,384},{576,480},{6... | collective-permute-start | bytes 98312 | tf_op jit(solution)/shard_map/ppermute | solution.py:37
  7.6 0.1 lt.28
  7.7 0.9 collective-permute-done
  8.6 11.3 %collective-permute-start.1 = (f32[3,1,2,8,128]{4,3,2,1,0:T(8,128)S(1)}, f32[3,1,2,8,128]{4,3,2,1,0:T(8,128)S(1)}, u32[]{:S(2)}, u32[]{:S(2)}) collective-permute-start(f32[3,1,2,8,128]{4,3,2,1,0:T(8,128)S(1)} %pad_maximum_fusion.2), channel_id=1, source_target_pairs={{0,84},{12,0},{24,12},{36,24},{48,36},{60,48},{72,60},{84,72},{1,8... | collective-permute-start | bytes 73736 | tf_op jit(solution)/shard_map/ppermute | solution.py:37
  19.9 0.1 compare_convert_fusion.1
  20.0 0.7 stack.43.refs_2_
  20.7 0.0 collective-permute-done.1
  20.8 10.4 %collective-permute-start.2 = (f32[3,5,1,8,128]{4,3,2,1,0:T(8,128)S(1)}, f32[3,5,1,8,128]{4,3,2,1,0:T(8,128)S(1)}, u32[]{:S(2)}, u32[]{:S(2)}) collective-permute-start(f32[3,5,1,8,128]{4,3,2,1,0:T(8,128)S(1)} %slice.155), channel_id=1, source_target_pairs={{0,11},{1,0},{2,1},{3,2},{4,3},{5,4},{6,5},{7,6},{8,7},{9,8},{10,9... | collective-permute-start | bytes 184328 | tf_op jit(solution)/shard_map/ppermute | solution.py:37
  31.2 0.0 copy-start.3
  31.2 0.0 copy-start.4
  31.2 0.0 copy-start.5
  31.2 0.6 copy-done.3
  31.8 0.0 copy-done.4
  31.8 0.0 copy-done.5
  31.8 0.6 pad_maximum_fusion.3.refs_0_
  32.4 10.3 %pair_sums.2 = (f32[16,8,128]{2,1,0:T(8,128)}, f32[8,128]{1,0:T(8,128)}) custom-call(f32[3,2]{1,0:T(4,128)} %pad_maximum_fusion.3.refs_0_, s32[176]{0:T(256)} %constant.93.refs_1_, f32[16,8,128]{2,1,0:T(8,128)} %stack.43.refs_2_), custom_call_target="tpu_custom_call" | custom-call | tf_op jit(solution)/shard_map/pair_sums/pallas_call | solution.py:272
  42.7 0.0 collective-permute-done.2
  42.7 0.7 pad_maximum_fusion
  43.4 15.3 %pair_sums.3 = (f32[45,8,128]{2,1,0:T(8,128)}, f32[32,128]{1,0:T(8,128)}) custom-call(f32[3,2]{1,0:T(4,128)} %pad_maximum_fusion.3.refs_0_, s32[272]{0:T(512)} %constant.92.refs_1_, f32[45,8,128]{2,1,0:T(8,128)} %bitcast.28, f32[8,128]{1,0:T(8,128)} %get-tuple-element.54.refs_3_), custom_call_target="tpu_custom_call" | custom-call | tf_op jit(solution)/shard_map/pair_sums/pallas_call | solution.py:272
  58.7 6.1 %all-to-all-start = ((f32[32,1,128]{2,1,0:T(1,128)}), f32[32,1,128]{2,1,0:T(1,128)S(1)}, u32[]{:S(2)}, u32[]{:S(2)}) async-start(f32[32,1,128]{2,1,0:T(1,128)} %bitcast.41), calls=%async_computation | async-start | bytes 32768 | tf_op jit(solution)/shard_map/all_to_all | solution.py:365
  64.8 0.9 fusion.3
  65.7 3.1 %collective-permute-start.3 = (f32[3,5,1,3,128]{4,2,1,0,3:T(1,128)S(1)}, f32[3,5,1,3,128]{4,2,1,0,3:T(1,128)S(1)}, u32[]{:S(2)}, u32[]{:S(2)}) collective-permute-start(f32[3,5,1,3,128]{4,2,1,0,3:T(1,128)S(1)} %copy.66), channel_id=1, source_target_pairs={{0,1},{1,2},{2,3},{3,4},{4,5},{5,6},{6,7},{7,8},{8,9},{9,10},{10,1... | collective-permute-start | bytes 69128 | tf_op jit(solution)/shard_map/ppermute | solution.py:37
  68.8 0.9 slice.168
  69.7 3.5 %all-to-all-done = f32[32,1,128]{2,1,0:T(1,128)S(1)} async-done(((f32[32,1,128]{2,1,0:T(1,128)}), f32[32,1,128]{2,1,0:T(1,128)S(1)}, u32[]{:S(2)}, u32[]{:S(2)}) %all-to-all-start) | async-done | bytes 16416 | tf_op jit(solution)/shard_map/all_to_all | solution.py:365
  73.3 0.1 reduce_sum.18
  73.3 3.1 %collective-permute-done.3 = f32[3,5,1,3,128]{4,2,1,0,3:T(1,128)S(1)} collective-permute-done((f32[3,5,1,3,128]{4,2,1,0,3:T(1,128)S(1)}, f32[3,5,1,3,128]{4,2,1,0,3:T(1,128)S(1)}, u32[]{:S(2)}, u32[]{:S(2)}) %collective-permute-start.3) | collective-permute-done | bytes 23072 | tf_op jit(solution)/shard_map/ppermute | solution.py:37
  76.4 0.1 scatter-add.10
  76.6 0.0 copy-start.1
  76.6 4.3 %collective-permute-start.4 = (f32[3,1,2,3,128]{4,2,1,0,3:T(2,128)S(1)}, f32[3,1,2,3,128]{4,2,1,0,3:T(2,128)S(1)}, u32[]{:S(2)}, u32[]{:S(2)}) collective-permute-start(f32[3,1,2,3,128]{4,2,1,0,3:T(2,128)S(1)} %slice.173), channel_id=1, source_target_pairs={{0,12},{12,24},{24,36},{36,48},{48,60},{60,72},{72,84},{84,0},{1,1... | collective-permute-start | bytes 27656 | tf_op jit(solution)/shard_map/ppermute | solution.py:37
  80.9 0.8 collective-permute-done.4
  81.7 3.1 %collective-permute-start.5 = (f32[1,4,2,3,128]{4,2,1,0,3:T(2,128)S(1)}, f32[1,4,2,3,128]{4,2,1,0,3:T(2,128)S(1)}, u32[]{:S(2)}, u32[]{:S(2)}) collective-permute-start(f32[1,4,2,3,128]{4,2,1,0,3:T(2,128)S(1)} %slice.176), channel_id=1, source_target_pairs={{0,96},{96,192},{192,288},{288,384},{384,480},{480,576},{576,672},... | collective-permute-start | bytes 36872 | tf_op jit(solution)/shard_map/ppermute | solution.py:37
  84.8 0.0 copy-done.1
  84.8 0.6 broadcast_in_dim.4
  85.4 8.2 %all-to-all-start.1 = ((f32[24,1,128]{2,1,0:T(1,128)}), f32[24,1,128]{2,1,0:T(1,128)S(1)}, u32[]{:S(2)}, u32[]{:S(2)}) async-start(f32[24,1,128]{2,1,0:T(1,128)} %broadcast_in_dim.4), calls=%async_computation.1 | async-start | bytes 24576 | tf_op jit(solution)/shard_map/all_to_all | solution.py:370
  93.7 0.0 collective-permute-done.5
  93.7 0.6 fusion
  94.4 8.8 %all-to-all-done.1 = f32[24,1,128]{2,1,0:T(1,128)S(1)} async-done(((f32[24,1,128]{2,1,0:T(1,128)}), f32[24,1,128]{2,1,0:T(1,128)S(1)}, u32[]{:S(2)}, u32[]{:S(2)}) %all-to-all-start.1) | async-done | bytes 12320 | tf_op jit(solution)/shard_map/all_to_all | solution.py:370
  103.2 0.5 slice_multiply_fusion
  (21 shorter events, 0.2 us)
Async XLA Ops:
  0.6 0.9 copy-start.2
  0.6 0.9 copy-start
  1.7 6.9 %collective-permute-start = (f32[1,4,2,8,128]{4,3,2,1,0:T(8,128)S(1)}, f32[1,4,2,8,128]{4,3,2,1,0:T(8,128)S(1)}, u32[]{:S(2)}, u32[]{:S(2)}) collective-permute-start(f32[1,4,2,8,128]{4,3,2,1,0:T(8,128)S(1)} %slice.167), channel_id=1, source_target_pairs={{0,672},{96,0},{192,96},{288,192},{384,288},{480,384},{576,480},{6... | collective-permute-start | bytes 98312 | tf_op jit(solution)/shard_map/ppermute | solution.py:37
  8.6 12.1 %collective-permute-start.1 = (f32[3,1,2,8,128]{4,3,2,1,0:T(8,128)S(1)}, f32[3,1,2,8,128]{4,3,2,1,0:T(8,128)S(1)}, u32[]{:S(2)}, u32[]{:S(2)}) collective-permute-start(f32[3,1,2,8,128]{4,3,2,1,0:T(8,128)S(1)} %pad_maximum_fusion.2), channel_id=1, source_target_pairs={{0,84},{12,0},{24,12},{36,24},{48,36},{60,48},{72,60},{84,72},{1,8... | collective-permute-start | bytes 73736 | tf_op jit(solution)/shard_map/ppermute | solution.py:37
  20.8 22.0 %collective-permute-start.2 = (f32[3,5,1,8,128]{4,3,2,1,0:T(8,128)S(1)}, f32[3,5,1,8,128]{4,3,2,1,0:T(8,128)S(1)}, u32[]{:S(2)}, u32[]{:S(2)}) collective-permute-start(f32[3,5,1,8,128]{4,3,2,1,0:T(8,128)S(1)} %slice.155), channel_id=1, source_target_pairs={{0,11},{1,0},{2,1},{3,2},{4,3},{5,4},{6,5},{7,6},{8,7},{9,8},{10,9... | collective-permute-start | bytes 184328 | tf_op jit(solution)/shard_map/ppermute | solution.py:37
  31.2 0.7 copy-start.3
  31.2 0.7 copy-start.4
  31.2 0.7 copy-start.5
  58.7 14.6 %all-to-all-start = ((f32[32,1,128]{2,1,0:T(1,128)}), f32[32,1,128]{2,1,0:T(1,128)S(1)}, u32[]{:S(2)}, u32[]{:S(2)}) async-start(f32[32,1,128]{2,1,0:T(1,128)} %bitcast.41), calls=%async_computation | async-start | bytes 32768 | tf_op jit(solution)/shard_map/all_to_all | solution.py:365
  65.7 10.7 %collective-permute-start.3 = (f32[3,5,1,3,128]{4,2,1,0,3:T(1,128)S(1)}, f32[3,5,1,3,128]{4,2,1,0,3:T(1,128)S(1)}, u32[]{:S(2)}, u32[]{:S(2)}) collective-permute-start(f32[3,5,1,3,128]{4,2,1,0,3:T(1,128)S(1)} %copy.66), channel_id=1, source_target_pairs={{0,1},{1,2},{2,3},{3,4},{4,5},{5,6},{6,7},{7,8},{8,9},{9,10},{10,1... | collective-permute-start | bytes 69128 | tf_op jit(solution)/shard_map/ppermute | solution.py:37
  76.6 8.2 %copy-start.1 = (f32[16,8,128]{2,1,0:T(8,128)S(1)}, f32[16,8,128]{2,1,0:T(8,128)}, u32[]{:S(2)}) copy-start(f32[16,8,128]{2,1,0:T(8,128)} %get-tuple-element.58) | copy-start | bytes 196612
  76.6 5.1 %collective-permute-start.4 = (f32[3,1,2,3,128]{4,2,1,0,3:T(2,128)S(1)}, f32[3,1,2,3,128]{4,2,1,0,3:T(2,128)S(1)}, u32[]{:S(2)}, u32[]{:S(2)}) collective-permute-start(f32[3,1,2,3,128]{4,2,1,0,3:T(2,128)S(1)} %slice.173), channel_id=1, source_target_pairs={{0,12},{12,24},{24,36},{36,48},{48,60},{60,72},{72,84},{84,0},{1,1... | collective-permute-start | bytes 27656 | tf_op jit(solution)/shard_map/ppermute | solution.py:37
  81.7 12.0 %collective-permute-start.5 = (f32[1,4,2,3,128]{4,2,1,0,3:T(2,128)S(1)}, f32[1,4,2,3,128]{4,2,1,0,3:T(2,128)S(1)}, u32[]{:S(2)}, u32[]{:S(2)}) collective-permute-start(f32[1,4,2,3,128]{4,2,1,0,3:T(2,128)S(1)} %slice.176), channel_id=1, source_target_pairs={{0,96},{96,192},{192,288},{288,384},{384,480},{480,576},{576,672},... | collective-permute-start | bytes 36872 | tf_op jit(solution)/shard_map/ppermute | solution.py:37
  85.4 17.7 %all-to-all-start.1 = ((f32[24,1,128]{2,1,0:T(1,128)}), f32[24,1,128]{2,1,0:T(1,128)S(1)}, u32[]{:S(2)}, u32[]{:S(2)}) async-start(f32[24,1,128]{2,1,0:T(1,128)} %broadcast_in_dim.4), calls=%async_computation.1 | async-start | bytes 24576 | tf_op jit(solution)/shard_map/all_to_all | solution.py:370
